TPU v7x, 32 devices: a whole 2x2x4 slice. The times are simulated.
32 devices in a mesh: pair: 8 (over z, x), sector: 4 (over y, core).
Axes of the slice: x: 2, y: 2, z: 4, core: 2. Of those that a mesh axis runs over, the one named last changes fastest.
Arguments:
- wave: bfloat16 [4, 1024, 1024], P('sector', 'pair'), may hold values from -6 to 6
- left_ops: bfloat16 [16, 4, 1024, 1024], P('pair', 'sector'), may hold values from -0.1875 to 0.1875
- right_ops: bfloat16 [16, 4, 1024, 1024], P('pair', 'sector'), may hold values from -0.046875 to 0.046875
- targets: int32 [16, 4], P('pair', 'sector'), may hold values from -1 to 3
- sector_sizes: int32 [4], replicated, may hold values from 256 to 1024
- pair_ids: int32 [16], P('pair'), may hold values from 0 to 15, each once
- pair_coefficients: float32 [16], replicated, may hold values from 0.25 to 2
Outputs:
- sigma_blocks: float32 [4, 1024, 1024], P('sector', 'pair')
Inputs may be any that keep to these rules, and one draw needn't show every extreme that they name: `pair_ids`: each orbital pair once.
All inputs are finite; a program needn't handle non-finite values.
Results may differ from a plain program's by a relative error of at most 0.0029.
Values may be sent and summed in bfloat16 or wider, within the bound.
A program may use at most 128 MiB of HBM per device.

v0:
```python
import functools

import jax
import jax.numpy as jnp
from jax import lax
from jax.experimental import pallas as pl
from jax.experimental.pallas import tpu as pltpu
from jax.sharding import PartitionSpec as P

MESH = pl.DeviceIdType.MESH
F32 = jnp.float32
LANES = 128
PLANE_DEPTH = 128
ROW_TILE = 512
PIECES = 2


def step_kernel(
    cfg, wave_ref, targets_ref, sizes_ref, ids_ref, coefs_ref, left_hbm, right_hbm, out_ref,
    wbuf, lbuf, rbuf, acc, left, own, psend, precv, weight_ref, wother,
    xs, xr, ys, yr, zs, zr, fsend, frecv, load_sem, sems_s, sems_r, line_s, line_r, gat_s, gat_r,
):
    Z, X, T, K, rows, block, groups, orders = cfg
    half = block // 2
    pair, sector = lax.axis_index("pair"), lax.axis_index("sector")
    z, x = pair // X, lax.rem(pair, X)
    y, c = sector // 2, lax.rem(sector, 2)

    def dev(zz=None, xx=None, yy=None, cc=None):
        zz, xx = z if zz is None else zz, x if xx is None else xx
        yy, cc = y if yy is None else yy, c if cc is None else cc
        return (zz * X + xx, yy * 2 + cc)

    x_dev, y_dev, c_dev = dev(xx=1 - x), dev(yy=1 - y), dev(cc=1 - c)
    up_dev, dn_dev = dev(zz=z + 1), dev(zz=z - 1)

    def loop(count, f):
        def one(i, carry):
            f(i)
            return carry

        lax.fori_loop(0, count, one, 0)

    has_up, has_dn = z + 1 < Z, z >= 1

    loads = []
    for k in range(K):
        loads.append(pltpu.make_async_copy(left_hbm.at[k], lbuf.at[k], load_sem.at[k]))
        loads.append(pltpu.make_async_copy(right_hbm.at[k], rbuf.at[k], load_sem.at[K + k]))
    for k in range(K):
        loads[2 * k].start()

    barrier = pltpu.get_barrier_semaphore()
    for other in (x_dev, y_dev, c_dev):
        pl.semaphore_signal(barrier, inc=1, device_id=other, device_id_type=MESH)

    def greet(zz):
        @pl.when(zz != z)
        def _():
            pl.semaphore_signal(barrier, inc=1, device_id=dev(zz=zz), device_id_type=MESH)

    loop(Z, greet)
    size = sizes_ref[sector]
    row_ids = pair * rows + lax.broadcasted_iota(jnp.int32, (rows, LANES), 0)
    lane_ids = lax.broadcasted_iota(jnp.int32, (rows, LANES), 1)

    def used(column):
        return ((row_ids < size) & (lane_ids + column < size)).astype(F32)

    for at in range(0, block, LANES):
        value = wave_ref[:, at : at + LANES].astype(F32) * used(at)
        wbuf[z, x, :, at : at + LANES] = value.astype(jnp.bfloat16)
    for k in range(K):
        factor = coefs_ref[ids_ref[k]]
        for t in range(T):
            chosen = jnp.where(targets_ref[k, 0] == t, factor, 0.0)
            weight_ref[k * T + t] = jnp.full((8, LANES), chosen, F32)
    for g in range(groups):
        for tc in range(2):
            zr[g][tc, z] = jnp.zeros((rows, LANES), jnp.bfloat16)
    pl.semaphore_wait(barrier, 3 + Z - 1)

    def remote(src, dst, ss, rs, device):
        return pltpu.make_async_remote_copy(
            src_ref=src, dst_ref=dst, send_sem=ss, recv_sem=rs, device_id=device, device_id_type=MESH
        )

    piece = rows // PIECES if rows % (16 * PIECES) == 0 else rows
    pieces = rows // piece

    def block_at(q, xx, p):
        return wbuf.at[q, xx, pl.ds(p * piece, piece)]

    def hop(q, way, p):
        device = (up_dev, dn_dev, x_dev)[way]
        return remote(block_at(q, x, p), block_at(q, x, p), gat_s.at[way, q, p], gat_r.at[q, x, p], device)

    def arrival(q, xx, p):
        return remote(block_at(q, xx, p), block_at(q, xx, p), gat_s.at[2, q, p], gat_r.at[q, xx, p], x_dev)

    def pass_on(q, ways, p):
        if 0 in ways:
            @pl.when(has_up)
            def _():
                hop(q, 0, p).start()

        if 1 in ways:
            @pl.when(has_dn)
            def _():
                hop(q, 1, p).start()

        hop(q, 2, p).start()

    for p in range(pieces):
        pass_on(z, (0, 1), p)
    weights_copy = remote(weight_ref, wother, sems_s.at[0], sems_r.at[0], c_dev)
    weights_copy.start()
    for k in range(K):
        loads[2 * k + 1].start()

    depth = X * rows
    planewise = depth % PLANE_DEPTH == 0
    tile = min(ROW_TILE, block)
    tiles = block // tile

    def multiply(q, first):
        plane = wbuf.at[q]

        def one(i, carry):
            k, at = i // tiles, pl.multiple_of(lax.rem(i, tiles) * tile, tile)
            cols = pl.ds(pl.multiple_of(q * depth, depth), depth)
            product = jnp.dot(
                lbuf[k, pl.ds(at, tile), cols], plane[...].reshape(depth, block), preferred_element_type=F32
            )
            if first:
                acc[k, pl.ds(at, tile), :] = product
            else:
                acc[k, pl.ds(at, tile), :] += product
            return carry

        lax.fori_loop(0, K * tiles, one, 0)

    def take_plane(q, first=False):
        for p in range(pieces):
            arrival(q, 1 - x, p).wait_recv()
        if planewise:
            multiply(q, first)

    for k in range(K):
        loads[2 * k].wait()

    def forward(d, carry):
        lo, hi = z - d, z + d
        for p in range(pieces):
            @pl.when(lo >= 0)
            def _():
                arrival(lo, x, p).wait_recv()
                pass_on(lo, (0,), p)

            @pl.when(hi < Z)
            def _():
                arrival(hi, x, p).wait_recv()
                pass_on(hi, (1,), p)

        @pl.when(d == 1)
        def _():
            take_plane(z, True)

        return carry

    lax.fori_loop(1, Z, forward, 0)

    def take_planes(d, carry):
        @pl.when(z - d >= 0)
        def _():
            take_plane(z - d)

        @pl.when(z + d < Z)
        def _():
            take_plane(z + d)

        return carry

    lax.fori_loop(1, Z, take_planes, 0)

    def finish_left(i, carry):
        k, at = i // tiles, pl.multiple_of(lax.rem(i, tiles) * tile, tile)
        if planewise:
            value = acc[k, pl.ds(at, tile), :]
        else:
            value = jnp.dot(
                lbuf[k, pl.ds(at, tile), :], wbuf[...].reshape(block, block), preferred_element_type=F32
            )
        left[k, pl.ds(at, tile), :] = value.astype(jnp.bfloat16)
        return carry

    lax.fori_loop(0, K * tiles, finish_left, 0)
    for k in range(K):
        loads[2 * k + 1].wait()

    width = 2 * LANES

    def second(part, side, dest):
        def one(i, carry):
            k, at = i // tiles, pl.multiple_of(lax.rem(i, tiles) * tile, tile)
            right_at = pl.multiple_of(side * half + part * width, width)
            term = lax.dot_general(
                left[k, pl.ds(at, tile), :], rbuf[k, pl.ds(right_at, width), :],
                (((1,), (1,)), ((), ())), preferred_element_type=F32,
            )
            for j in range(2):
                dest[2 * part + j, k, pl.ds(at, tile), :] = term[:, j * LANES : (j + 1) * LANES].astype(dest.dtype)
            return carry

        lax.fori_loop(0, K * tiles, one, 0)

    def part_copy(part):
        span = pl.ds(2 * part, 2)
        return remote(psend.at[span], precv.at[span], sems_s.at[1 + part], sems_r.at[1 + part], c_dev)

    base = 1 + groups // 2

    def step_copy(g, number, tc):
        letter = orders[g][number]
        s, r = ((xs, xr), (ys, yr))["xy".index(letter)]
        at = base + 4 * g + 2 * number + tc
        return remote(s[g].at[tc], r[g].at[tc], sems_s.at[at], sems_r.at[at], x_dev if letter == "x" else y_dev)

    def chip_sum(g, ty, tc, zz, xx):
        at = pl.ds(pl.multiple_of((zz * X + xx) * rows, rows), rows)
        t = ty * 2 + tc
        total = None
        for k in range(K):
            mine = own[g, k, at, :] * weight_ref[k * T + t, 0:1, :]
            theirs = precv[g, k, at, :].astype(F32) * wother[k * T + t, 0:1, :]
            total = mine + theirs if total is None else total + mine + theirs
        return total

    def x_first(g, tc):
        def one(zz):
            for ty in range(2):
                xs[g][tc, ty, zz] = chip_sum(g, ty, tc, zz, 1 - x).astype(jnp.bfloat16)

        loop(Z, one)
        step_copy(g, 0, tc).start()

    def y_first(g, tc):
        def one(zz):
            for xx in range(2):
                ys[g][tc, zz, xx] = chip_sum(g, 1 - y, tc, zz, xx).astype(jnp.bfloat16)

        loop(Z, one)
        step_copy(g, 0, tc).start()

    def y_second(g, tc):
        step_copy(g, 0, tc).wait_recv()

        def one(zz):
            value = chip_sum(g, 1 - y, tc, zz, x) + xr[g][tc, 1 - y, zz].astype(F32)
            ys[g][tc, zz] = value.astype(jnp.bfloat16)

        loop(Z, one)
        step_copy(g, 1, tc).start()

    def x_second(g, tc):
        step_copy(g, 0, tc).wait_recv()

        def one(zz):
            value = chip_sum(g, y, tc, zz, 1 - x) + yr[g][tc, zz, 1 - x].astype(F32)
            xs[g][tc, zz] = value.astype(jnp.bfloat16)

        loop(Z, one)
        step_copy(g, 1, tc).start()

    def plane_sum(g, tc, zz):
        value = chip_sum(g, y, tc, zz, x)
        if orders[g][0] == "x":
            return value + xr[g][tc, y, zz].astype(F32) + yr[g][tc, zz].astype(F32)
        return value + yr[g][tc, zz, x].astype(F32) + xr[g][tc, zz].astype(F32)

    def line_copy(g, tc, zz):
        return remote(
            zs[g].at[tc, zz], zr[g].at[tc, z], line_s.at[g, tc, zz], line_r.at[g, tc, z], dev(zz=zz)
        )

    def line_arrival(g, tc, zz):
        return remote(
            zs[g].at[tc, zz], zr[g].at[tc, zz], line_s.at[g, tc, zz], line_r.at[g, tc, zz], dev(zz=zz)
        )

    def line(g, tc):
        step_copy(g, 1, tc).wait_recv()

        def one(j):
            zz = lax.rem(z + 1 + j, Z)
            zs[g][tc, zz] = plane_sum(g, tc, zz).astype(jnp.bfloat16)
            line_copy(g, tc, zz).start()

        loop(Z - 1, one)

    def total(g, tc):
        value = plane_sum(g, tc, z)
        if Z <= 8:
            for zz in range(Z):
                value = value + zr[g][tc, zz].astype(F32)
            return value
        return lax.fori_loop(0, Z, lambda zz, v: v + zr[g][tc, zz].astype(F32), value)

    def final_copy(g):
        at = base + 4 * groups + g
        return remote(fsend.at[g], frecv.at[g], sems_s.at[at], sems_r.at[at], c_dev)

    def finish(g):
        def wait(j):
            for tc in range(2):
                line_arrival(g, tc, lax.rem(z + 1 + j, Z)).wait_recv()

        loop(Z - 1, wait)
        fsend[g] = total(g, 1 - c)
        final_copy(g).start()
        at = pl.multiple_of(c * half + g * LANES, LANES)
        out_ref[:, pl.ds(at, LANES)] = total(g, c) * used(at)

    def first(i):
        x_first(2 * (i // 2), i % 2)
        y_first(2 * (i // 2) + 1, i % 2)

    def next_step(i):
        y_second(2 * (i // 2), i % 2)
        x_second(2 * (i // 2) + 1, i % 2)

    def lines(i):
        line(2 * (i // 2), i % 2)
        line(2 * (i // 2) + 1, i % 2)

    parts = groups // 2
    rounds = groups
    second(0, 1 - c, psend)
    part_copy(0).start()
    second(0, c, own)
    weights_copy.wait_recv()
    for i in range(rounds):
        part = i // 2
        if i % 2 == 0:
            if part + 1 < parts:
                second(part + 1, 1 - c, psend)
                part_copy(part + 1).start()
            part_copy(part).wait_recv()
        first(i)
        if i % 2 == 1 and part + 1 < parts:
            second(part + 1, c, own)
        if i >= 1:
            next_step(i - 1)
        if i >= 2:
            lines(i - 2)
    next_step(rounds - 1)
    lines(rounds - 2)
    for g in range(groups - 2):
        finish(g)
    lines(rounds - 1)
    for g in range(groups - 2, groups):
        finish(g)
    for g in range(groups):
        final_copy(g).wait_recv()
        at = pl.multiple_of((1 - c) * half + g * LANES, LANES)
        out_ref[:, pl.ds(at, LANES)] = frecv[g] * used(at)

    def drain(q):
        for p in range(pieces):
            @pl.when(jnp.logical_and(has_up, q <= z))
            def _():
                hop(q, 0, p).wait_send()

            @pl.when(jnp.logical_and(has_dn, q >= z))
            def _():
                hop(q, 1, p).wait_send()

            hop(q, 2, p).wait_send()

    loop(Z, drain)
    weights_copy.wait_send()
    for part in range(parts):
        part_copy(part).wait_send()
    for g in range(groups):
        final_copy(g).wait_send()
        for tc in range(2):
            step_copy(g, 0, tc).wait_send()
            step_copy(g, 1, tc).wait_send()

            def drain_line(j, g=g, tc=tc):
                line_copy(g, tc, lax.rem(z + 1 + j, Z)).wait_send()

            loop(Z - 1, drain_line)


def kernel_entry(cfg, *refs):
    groups = cfg[6]
    ins, scratch = refs[:8], list(refs[8:])
    plain = scratch[:10]
    per_group = [scratch[10 + n * groups : 10 + (n + 1) * groups] for n in range(6)]
    step_kernel(cfg, *ins, *plain, *per_group, *scratch[10 + 6 * groups :])


def body(wave, left_ops, right_ops, targets, sector_sizes, pair_ids, pair_coefficients):
    block = wave.shape[2]
    rows = wave.shape[1]
    K = left_ops.shape[0]
    T = sector_sizes.shape[0]
    pairs = lax.axis_size("pair")
    X = 2
    Z = pairs // X
    half = block // 2
    groups = half // LANES
    orders = tuple(("xyz", "yxz")[g % 2] for g in range(groups))
    bf = jnp.bfloat16
    xs, xr, ys, yr, zs, zr = [], [], [], [], [], []
    for order in orders:
        tail = (rows, LANES)
        x_shape, y_shape = {"x": ((2, 2, Z), (2, Z)), "y": ((2, Z), (2, Z, X))}[order[0]]
        for where, shape in ((xs, x_shape), (xr, x_shape), (ys, y_shape), (yr, y_shape), (zs, (2, Z)), (zr, (2, Z))):
            where.append(pltpu.VMEM(shape + tail, bf))
    count = 1 + groups // 2 + 5 * groups
    dma = pltpu.SemaphoreType.DMA
    cfg = (Z, X, T, K, rows, block, groups, orders)
    planewise = (X * rows) % PLANE_DEPTH == 0
    vmem, anywhere = pl.BlockSpec(memory_space=pltpu.VMEM), pl.BlockSpec(memory_space=pl.ANY)
    smem = pl.BlockSpec(memory_space=pltpu.SMEM)
    out = pl.pallas_call(
        functools.partial(kernel_entry, cfg),
        out_shape=jax.ShapeDtypeStruct((rows, block), F32),
        in_specs=[vmem, smem, smem, smem, smem, anywhere, anywhere],
        out_specs=vmem,
        scratch_shapes=[
            pltpu.VMEM((Z, X, rows, block), bf),
            pltpu.VMEM((K, block, block), bf),
            pltpu.VMEM((K, block, block), bf),
            pltpu.VMEM((K, block, block) if planewise else (8, LANES), F32),
            pltpu.VMEM((K, block, block), bf),
            pltpu.VMEM((groups, K, block, LANES), F32),
            pltpu.VMEM((groups, K, block, LANES), F32),
            pltpu.VMEM((groups, K, block, LANES), F32),
            pltpu.VMEM((K * T, 8, LANES), F32),
            pltpu.VMEM((K * T, 8, LANES), F32),
            *xs, *xr, *ys, *yr, *zs, *zr,
            pltpu.VMEM((groups, rows, LANES), F32),
            pltpu.VMEM((groups, rows, LANES), F32),
            dma((2 * K,)), dma((count,)), dma((count,)),
            dma((groups, 2, Z)), dma((groups, 2, Z)), dma((3, Z, PIECES)), dma((Z, X, PIECES)),
        ],
        compiler_params=pltpu.CompilerParams(
            collective_id=0, has_side_effects=True, vmem_limit_bytes=60 * 1024 * 1024
        ),
        name="sigma_step",
    )(wave[0], targets, sector_sizes, pair_ids, pair_coefficients, left_ops[:, 0], right_ops[:, 0])
    return out[None]


def solution(mesh):
    placed = (
        P("sector", "pair", None),
        P("pair", "sector", None, None),
        P("pair", "sector", None, None),
        P("pair", "sector"),
        P(),
        P("pair"),
        P(),
    )
    return jax.shard_map(
        body, mesh=mesh, in_specs=placed, out_specs=P("sector", "pair", None), check_vma=False
    )
```

profile of v0, /device:TPU:0, one launch (start us, length us, event | category | flops | bytes accessed | tf_op | source)
XLA Modules:
  0.0 90.8 jit_solution(9135167624313654304)
XLA Ops:
  0.0 1.3 %copy.8.refs_1_ = s32[2,1]{1,0:T(2,128)} copy(s32[2,1]{0,1:T(1,128)} %param.10) | data formatting | bytes 16 | tf_op args[3]
  1.3 87.6 %sigma_step.1 = f32[128,1024]{1,0:T(8,128)} custom-call(bf16[128,1024]{1,0:T(8,128)(2,1)} %bitcast.7, s32[2,1]{1,0:T(2,128)} %copy.8.refs_1_, s32[4]{0:T(128)} %refs_2_.1, s32[2]{0:T(128)} %refs_3_.1, f32[16]{0:T(128)} %refs_4_.1, bf16[2,1024,1024]{2,1,0:T(8,128)(2,1)} %bitcast.4, bf16[2,1024,1024]{2,1,0:T(8,128)(2,1)} %bitcast.5), custom_call_target="tpu_custom_call" | custom-call | tf_op jit(solution)/shard_map/sigma_step/pallas_call | solution.py:428
  88.9 1.9 %copy.10 = f32[1,128,1024]{2,1,0:T(8,128)} copy(f32[1,128,1024]{2,1,0:T(8,128)} %bitcast.6) | data formatting | bytes 1048576
where the time goes:
time: 91.2 us; the launch traced here: 90.8 us
  Pallas kernels  87.6 us (96%)
  local copies, waits for them, and re-layouts  3.18 us (3%)
    pallas_call x1, Pallas kernels, body(): pl.pallas_call(functools.partial(kernel_entry, cfg), out_shape=jax.ShapeD...  87.6 us
    unnamed x2, local copies, waits for them, and re-layouts  3.18 us

commit v1 on v0

--- a/solution.py
+++ b/solution.py
@@ -13,11 +13,12 @@
 PLANE_DEPTH = 128
 ROW_TILE = 512
 PIECES = 2
+VMEM_LIMIT = 48 * 1024 * 1024
 
 
 def step_kernel(
-    cfg, wave_ref, targets_ref, sizes_ref, ids_ref, coefs_ref, left_hbm, right_hbm, out_ref,
-    wbuf, lbuf, rbuf, acc, left, own, psend, precv, weight_ref, wother,
+    cfg, wave_hbm, targets_ref, sizes_ref, ids_ref, coefs_ref, left_hbm, right_hbm, out_ref,
+    wave_ref, wbuf, lbuf, rbuf, acc, left, own, psend, precv, weight_ref, wother,
     xs, xr, ys, yr, zs, zr, fsend, frecv, load_sem, sems_s, sems_r, line_s, line_r, gat_s, gat_r,
 ):
     Z, X, T, K, rows, block, groups, orders = cfg
@@ -47,38 +48,43 @@
     for k in range(K):
         loads.append(pltpu.make_async_copy(left_hbm.at[k], lbuf.at[k], load_sem.at[k]))
         loads.append(pltpu.make_async_copy(right_hbm.at[k], rbuf.at[k], load_sem.at[K + k]))
-    for k in range(K):
-        loads[2 * k].start()
-
     barrier = pltpu.get_barrier_semaphore()
     for other in (x_dev, y_dev, c_dev):
         pl.semaphore_signal(barrier, inc=1, device_id=other, device_id_type=MESH)
 
-    def greet(zz):
-        @pl.when(zz != z)
-        def _():
-            pl.semaphore_signal(barrier, inc=1, device_id=dev(zz=zz), device_id_type=MESH)
-
-    loop(Z, greet)
-    size = sizes_ref[sector]
-    row_ids = pair * rows + lax.broadcasted_iota(jnp.int32, (rows, LANES), 0)
-    lane_ids = lax.broadcasted_iota(jnp.int32, (rows, LANES), 1)
-
-    def used(column):
-        return ((row_ids < size) & (lane_ids + column < size)).astype(F32)
-
-    for at in range(0, block, LANES):
-        value = wave_ref[:, at : at + LANES].astype(F32) * used(at)
-        wbuf[z, x, :, at : at + LANES] = value.astype(jnp.bfloat16)
+    wave_load = pltpu.make_async_copy(wave_hbm, wave_ref, load_sem.at[2 * K])
+    wave_load.start()
+
+    @pl.when(has_up)
+    def _():
+        pl.semaphore_signal(barrier, inc=1, device_id=up_dev, device_id_type=MESH)
+
+    @pl.when(has_dn)
+    def _():
+        pl.semaphore_signal(barrier, inc=1, device_id=dn_dev, device_id_type=MESH)
+
     for k in range(K):
         factor = coefs_ref[ids_ref[k]]
         for t in range(T):
-            chosen = jnp.where(targets_ref[k, 0] == t, factor, 0.0)
+            chosen = jnp.where(targets_ref[k] == t, factor, 0.0)
             weight_ref[k * T + t] = jnp.full((8, LANES), chosen, F32)
     for g in range(groups):
         for tc in range(2):
             zr[g][tc, z] = jnp.zeros((rows, LANES), jnp.bfloat16)
-    pl.semaphore_wait(barrier, 3 + Z - 1)
+    for k in range(K):
+        loads[2 * k].start()
+    size = sizes_ref[sector]
+    row_ids = pair * rows + lax.broadcasted_iota(jnp.int32, (rows, LANES), 0)
+    lane_ids = lax.broadcasted_iota(jnp.int32, (rows, LANES), 1)
+
+    def used(column):
+        return ((row_ids < size) & (lane_ids + column < size)).astype(F32)
+
+    wave_load.wait()
+    for at in range(0, block, LANES):
+        value = wave_ref[:, at : at + LANES].astype(F32) * used(at)
+        wbuf[z, x, :, at : at + LANES] = value.astype(jnp.bfloat16)
+    pl.semaphore_wait(barrier, 3 + has_up.astype(jnp.int32) + has_dn.astype(jnp.int32))
 
     def remote(src, dst, ss, rs, device):
         return pltpu.make_async_remote_copy(
@@ -396,9 +402,9 @@
 def kernel_entry(cfg, *refs):
     groups = cfg[6]
     ins, scratch = refs[:8], list(refs[8:])
-    plain = scratch[:10]
-    per_group = [scratch[10 + n * groups : 10 + (n + 1) * groups] for n in range(6)]
-    step_kernel(cfg, *ins, *plain, *per_group, *scratch[10 + 6 * groups :])
+    plain = scratch[:11]
+    per_group = [scratch[11 + n * groups : 11 + (n + 1) * groups] for n in range(6)]
+    step_kernel(cfg, *ins, *plain, *per_group, *scratch[11 + 6 * groups :])
 
 
 def body(wave, left_ops, right_ops, targets, sector_sizes, pair_ids, pair_coefficients):
@@ -423,14 +429,15 @@
     dma = pltpu.SemaphoreType.DMA
     cfg = (Z, X, T, K, rows, block, groups, orders)
     planewise = (X * rows) % PLANE_DEPTH == 0
-    vmem, anywhere = pl.BlockSpec(memory_space=pltpu.VMEM), pl.BlockSpec(memory_space=pl.ANY)
+    vmem, hbm = pl.BlockSpec(memory_space=pltpu.VMEM), pl.BlockSpec(memory_space=pltpu.HBM)
     smem = pl.BlockSpec(memory_space=pltpu.SMEM)
     out = pl.pallas_call(
         functools.partial(kernel_entry, cfg),
         out_shape=jax.ShapeDtypeStruct((rows, block), F32),
-        in_specs=[vmem, smem, smem, smem, smem, anywhere, anywhere],
+        in_specs=[hbm, smem, smem, smem, smem, hbm, hbm],
         out_specs=vmem,
         scratch_shapes=[
+            pltpu.VMEM((rows, block), bf),
             pltpu.VMEM((Z, X, rows, block), bf),
             pltpu.VMEM((K, block, block), bf),
             pltpu.VMEM((K, block, block), bf),
@@ -444,14 +451,14 @@
             *xs, *xr, *ys, *yr, *zs, *zr,
             pltpu.VMEM((groups, rows, LANES), F32),
             pltpu.VMEM((groups, rows, LANES), F32),
-            dma((2 * K,)), dma((count,)), dma((count,)),
+            dma((2 * K + 1,)), dma((count,)), dma((count,)),
             dma((groups, 2, Z)), dma((groups, 2, Z)), dma((3, Z, PIECES)), dma((Z, X, PIECES)),
         ],
         compiler_params=pltpu.CompilerParams(
-            collective_id=0, has_side_effects=True, vmem_limit_bytes=60 * 1024 * 1024
+            collective_id=0, has_side_effects=True, vmem_limit_bytes=VMEM_LIMIT
         ),
         name="sigma_step",
-    )(wave[0], targets, sector_sizes, pair_ids, pair_coefficients, left_ops[:, 0], right_ops[:, 0])
+    )(wave[0], targets.reshape(-1), sector_sizes, pair_ids, pair_coefficients, left_ops[:, 0], right_ops[:, 0])
     return out[None]
 
 

time: 91.2 us -> 93.4 us (1.024)
  local copies, waits for them, and re-layouts: 3.18 us -> 6.55 us
  Pallas kernels: 87.6 us -> 86.4 us
    unnamed x2 -> x13, local copies, waits for them, and re-layouts: 3.18 us -> 6.55 us
    pallas_call x1, Pallas kernels: 87.6 us -> 86.4 us  [body(): pl.pallas_call(functools.partial(kernel_entry, cfg), out_shape=jax.ShapeD...]
where the time goes in v1:
time: 93.4 us; the launch traced here: 93 us
  Pallas kernels  86.4 us (93%)
  local copies, waits for them, and re-layouts  6.55 us (7%)
    pallas_call x1, Pallas kernels, body(): pl.pallas_call(functools.partial(kernel_entry, cfg), out_shape=jax.ShapeD...  86.4 us
    unnamed x13, local copies, waits for them, and re-layouts  6.55 us

profile of v1, /device:TPU:0, one launch (start us, length us, event | category | flops | bytes accessed | tf_op | source)
XLA Modules:
  0.0 93.0 jit_solution(1076409850138238484)
XLA Ops:
  0.0 0.0 copy-start
  0.0 2.2 %copy-done = bf16[2,1,1024,1024]{3,2,1,0:T(8,128)(2,1)S(1)} copy-done((bf16[2,1,1024,1024]{3,2,1,0:T(8,128)(2,1)S(1)}, bf16[2,1,1024,1024]{3,2,1,0:T(8,128)(2,1)}, u32[]{:S(2)}) %copy-start) | copy-done | bytes 4194328
  2.2 0.0 copy-start.1
  2.2 0.9 %copy-done.1 = bf16[1,128,1024]{2,1,0:T(8,128)(2,1)S(1)} copy-done((bf16[1,128,1024]{2,1,0:T(8,128)(2,1)S(1)}, bf16[1,128,1024]{2,1,0:T(8,128)(2,1)}, u32[]{:S(2)}) %copy-start.1) | copy-done | bytes 262168
  3.1 0.0 copy-start.2
  3.1 0.7 copy-done.2
  3.8 0.0 copy-start.3
  3.8 0.7 copy-done.3
  4.5 0.0 copy-start.4
  4.5 0.7 copy-done.4
  5.1 0.0 copy-start.5
  5.1 0.7 copy-done.5
  5.8 86.4 %sigma_step.1 = f32[128,1024]{1,0:T(8,128)S(1)} custom-call(bf16[128,1024]{1,0:T(8,128)(2,1)S(1)} %bitcast.7, s32[2]{0:T(128)S(1)} %bitcast.8, s32[4]{0:T(128)S(1)} %copy-done.3, s32[2]{0:T(128)S(1)} %copy-done.4, f32[16]{0:T(128)S(1)} %copy-done.5, bf16[2,1024,1024]{2,1,0:T(8,128)(2,1)S(1)} %bitcast.5, bf16[2,1024,1024]{2,1,0:T(8,128)(2,1)} %bitcast.9), custom_call_target="tpu_custom_call" | custom-call | tf_op jit(solution)/shard_map/sigma_step/pallas_call | solution.py:434
  92.2 0.8 copy.9
Async XLA Ops:
  0.0 2.2 %copy-start = (bf16[2,1,1024,1024]{3,2,1,0:T(8,128)(2,1)S(1)}, bf16[2,1,1024,1024]{3,2,1,0:T(8,128)(2,1)}, u32[]{:S(2)}) copy-start(bf16[2,1,1024,1024]{3,2,1,0:T(8,128)(2,1)} %param.8) | copy-start | bytes 12582916
  2.2 0.9 %copy-start.1 = (bf16[1,128,1024]{2,1,0:T(8,128)(2,1)S(1)}, bf16[1,128,1024]{2,1,0:T(8,128)(2,1)}, u32[]{:S(2)}) copy-start(bf16[1,128,1024]{2,1,0:T(8,128)(2,1)} %param.7) | copy-start | bytes 786436
  3.1 0.7 copy-start.2
  3.8 0.7 copy-start.3
  4.5 0.7 copy-start.4
  5.1 0.7 copy-start.5

commit v2 on v1

v2 whole, which is shorter than its diff:
```python
import functools

import jax
import jax.numpy as jnp
from jax import lax
from jax.experimental import pallas as pl
from jax.experimental.pallas import tpu as pltpu
from jax.sharding import PartitionSpec as P

MESH = pl.DeviceIdType.MESH
F32 = jnp.float32
BF16 = jnp.bfloat16
LANES = 128
PLANE_DEPTH = 128
ROW_TILE = 512
PIECES = 2
VMEM_LIMIT = 48 * 1024 * 1024
KINDS = ("xs", "xr", "ys", "yr", "zs", "zr")


def plan(groups, split):
    if split == 2:
        pairs = [[(g, tc, h) for h in range(2)] for g in range(groups) for tc in range(2)]
    else:
        pairs = [[(g, tc, 0) for tc in range(2)] for g in range(groups)]
    orders = [("zxy", "zyx") if n == 1 else ("xyz", "yxz") for n in range(len(pairs))]
    return [[unit + (order,) for unit, order in zip(pair, way)] for pair, way in zip(pairs, orders)]


def step_kernel(
    cfg, wave_hbm, targets_ref, sizes_ref, ids_ref, coefs_ref, left_hbm, right_hbm, out_ref,
    wave_ref, wbuf, lbuf, rbuf, acc, left, own, psend, precv, weight_ref, wother, fsend, frecv,
    load_sem, sems_s, sems_r, line_s, line_r, gat_s, gat_r, relay_s, bufs,
):
    Z, X, T, K, rows, block, groups, split, pairs = cfg
    units = [unit for pair in pairs for unit in pair]
    half = block // 2
    pair, sector = lax.axis_index("pair"), lax.axis_index("sector")
    z, x = pair // X, lax.rem(pair, X)
    y, c = sector // 2, lax.rem(sector, 2)

    def dev(zz=None, xx=None, yy=None, cc=None):
        zz, xx = z if zz is None else zz, x if xx is None else xx
        yy, cc = y if yy is None else yy, c if cc is None else cc
        return (zz * X + xx, yy * 2 + cc)

    x_dev, y_dev, c_dev = dev(xx=1 - x), dev(yy=1 - y), dev(cc=1 - c)
    up_dev, dn_dev = dev(zz=z + 1), dev(zz=z - 1)

    def loop(count, f):
        def one(i, carry):
            f(i)
            return carry

        lax.fori_loop(0, count, one, 0)

    has_up, has_dn = z + 1 < Z, z >= 1

    left_loads = [pltpu.make_async_copy(left_hbm.at[k], lbuf.at[k], load_sem.at[k]) for k in range(K)]
    right_loads = []
    for k in range(K):
        for g in range(groups):
            for j in range(2):
                at = pl.multiple_of((1 - c if j == 0 else c) * half + g * LANES, LANES)
                right_loads.append(
                    pltpu.make_async_copy(
                        right_hbm.at[k, pl.ds(at, LANES)], rbuf.at[k, g, j],
                        load_sem.at[K + 1 + (k * groups + g) * 2 + j],
                    )
                )

    barrier = pltpu.get_barrier_semaphore()
    for other in (x_dev, y_dev, c_dev):
        pl.semaphore_signal(barrier, inc=1, device_id=other, device_id_type=MESH)

    wave_load = pltpu.make_async_copy(wave_hbm, wave_ref, load_sem.at[K])
    wave_load.start()

    @pl.when(has_up)
    def _():
        pl.semaphore_signal(barrier, inc=1, device_id=up_dev, device_id_type=MESH)

    @pl.when(has_dn)
    def _():
        pl.semaphore_signal(barrier, inc=1, device_id=dn_dev, device_id_type=MESH)

    for k in range(K):
        factor = coefs_ref[ids_ref[k]]
        for t in range(T):
            chosen = jnp.where(targets_ref[k] == t, factor, 0.0)
            weight_ref[k * T + t] = jnp.full((8, LANES), chosen, F32)
    for n in range(len(units)):
        mine = bufs["zr"][n].at[z]
        mine[...] = jnp.zeros(mine.shape, BF16)
    for copy in left_loads:
        copy.start()
    size = sizes_ref[sector]

    def used(column, start=0, count=rows):
        row_ids = pair * rows + start + lax.broadcasted_iota(jnp.int32, (count, LANES), 0)
        lane_ids = column + lax.broadcasted_iota(jnp.int32, (count, LANES), 1)
        return ((row_ids < size) & (lane_ids < size)).astype(F32)

    wave_load.wait()
    for at in range(0, block, LANES):
        value = wave_ref[:, at : at + LANES].astype(F32) * used(at)
        wbuf[z, x, :, at : at + LANES] = value.astype(jnp.bfloat16)
    pl.semaphore_wait(barrier, 3 + has_up.astype(jnp.int32) + has_dn.astype(jnp.int32))

    def remote(src, dst, ss, rs, device):
        return pltpu.make_async_remote_copy(
            src_ref=src, dst_ref=dst, send_sem=ss, recv_sem=rs, device_id=device, device_id_type=MESH
        )

    piece = rows // PIECES if rows % (16 * PIECES) == 0 else rows
    pieces = rows // piece

    def block_at(q, xx, p):
        return wbuf.at[q, xx, pl.ds(p * piece, piece)]

    def hop(q, way, p):
        device = (up_dev, dn_dev, x_dev)[way]
        return remote(block_at(q, x, p), block_at(q, x, p), gat_s.at[way, q, p], gat_r.at[q, x, p], device)

    def arrival(q, xx, p):
        return remote(block_at(q, xx, p), block_at(q, xx, p), gat_s.at[2, q, p], gat_r.at[q, xx, p], x_dev)

    relayed = Z >= 3 and pieces >= 2
    last = pieces - 1

    def skips_x(q, p):
        if not relayed or p != last:
            return jnp.bool_(False)
        return ((z == 0) & (q == 1)) | ((z == Z - 1) & (q == Z - 2))

    def relay(way):
        device = (up_dev, dn_dev)[way]
        block_there = block_at(z, 1 - x, last)
        return remote(block_there, block_there, relay_s.at[way], gat_r.at[z, 1 - x, last], device)

    def relays(f):
        if relayed:
            @pl.when(z == Z - 2)
            def _():
                f(relay(0))

            @pl.when(z == 1)
            def _():
                f(relay(1))

    def pass_on(q, ways, p):
        if 0 in ways:
            @pl.when(has_up)
            def _():
                hop(q, 0, p).start()

        if 1 in ways:
            @pl.when(has_dn)
            def _():
                hop(q, 1, p).start()

        @pl.when(jnp.logical_not(skips_x(q, p)))
        def _():
            hop(q, 2, p).start()

    for p in range(pieces):
        pass_on(z, (0, 1), p)
    weights_copy = remote(weight_ref, wother, sems_s.at[0], sems_r.at[0], c_dev)
    weights_copy.start()
    for copy in right_loads:
        copy.start()

    depth = X * rows
    planewise = depth % PLANE_DEPTH == 0
    tile = min(ROW_TILE, block)
    tiles = block // tile

    def multiply(q, stage):
        plane = wbuf.at[q]

        def one(i, carry):
            k, at = i // tiles, pl.multiple_of(lax.rem(i, tiles) * tile, tile)
            cols = pl.ds(pl.multiple_of(q * depth, depth), depth)
            product = jnp.dot(
                lbuf[k, pl.ds(at, tile), cols], plane[...].reshape(depth, block), preferred_element_type=F32
            )
            if stage == "only":
                left[k, pl.ds(at, tile), :] = product.astype(BF16)
            elif stage == "first":
                acc[k, pl.ds(at, tile), :] = product
            elif stage == "middle":
                acc[k, pl.ds(at, tile), :] += product
            else:
                left[k, pl.ds(at, tile), :] = (acc[k, pl.ds(at, tile), :] + product).astype(BF16)
            return carry

        lax.fori_loop(0, K * tiles, one, 0)

    def take_plane(q, stage):
        for p in range(pieces):
            arrival(q, 1 - x, p).wait_recv()
        if stage in ("first", "only"):
            relays(lambda copy: copy.start())
        if planewise:
            multiply(q, stage)

    for copy in left_loads:
        copy.wait()

    def forward(d, carry):
        lo, hi = z - d, z + d
        for p in range(pieces):
            @pl.when(lo >= 0)
            def _():
                arrival(lo, x, p).wait_recv()
                pass_on(lo, (0,), p)

            @pl.when(hi < Z)
            def _():
                arrival(hi, x, p).wait_recv()
                pass_on(hi, (1,), p)

        @pl.when(d == 1)
        def _():
            take_plane(z, "first")

        return carry

    if Z == 1:
        take_plane(z, "only")
    lax.fori_loop(1, Z, forward, 0)
    near = jnp.minimum(z, Z - 1 - z)

    def plane_by_distance(i):
        d = (i + 1) // 2
        both = jnp.where(lax.rem(i, 2) == 1, z - d, z + d)
        return jnp.where(i <= 2 * near, both, jnp.where(z > near, z - (i - near), z + (i - near)))

    def take_planes(i, carry):
        take_plane(plane_by_distance(i), "middle")
        return carry

    lax.fori_loop(1, Z - 1, take_planes, 0)
    if Z > 1:
        take_plane(plane_by_distance(jnp.int32(Z - 1)), "last")

    def whole_left(i, carry):
        k, at = i // tiles, pl.multiple_of(lax.rem(i, tiles) * tile, tile)
        value = jnp.dot(
            lbuf[k, pl.ds(at, tile), :], wbuf[...].reshape(block, block), preferred_element_type=F32
        )
        left[k, pl.ds(at, tile), :] = value.astype(BF16)
        return carry

    if not planewise:
        lax.fori_loop(0, K * tiles, whole_left, 0)
    for copy in right_loads:
        copy.wait()

    def core_copy(g, k):
        at = 1 + g * K + k
        return remote(psend.at[g, k], precv.at[g, k], sems_s.at[at], sems_r.at[at], c_dev)

    def second(g, k):
        def one(i, carry):
            at = pl.multiple_of(i * tile, tile)
            term = lax.dot_general(
                left[k, pl.ds(at, tile), :], rbuf[k, g].reshape(2 * LANES, block),
                (((1,), (1,)), ((), ())), preferred_element_type=F32,
            )
            psend[g, k, pl.ds(at, tile), :] = term[:, :LANES].astype(BF16)
            own[g, k, pl.ds(at, tile), :] = term[:, LANES:]
            return carry

        lax.fori_loop(0, tiles, one, 0)
        core_copy(g, k).start()

    part = rows // split

    def chip_sum(n, ty, zz, xx):
        g, tc, h, _ = units[n]
        at = pl.ds(pl.multiple_of((zz * X + xx) * rows + h * part, part), part)
        t = ty * 2 + tc
        total = None
        for k in range(K):
            mine = own[g, k, at, :] * weight_ref[k * T + t, 0:1, :]
            theirs = precv[g, k, at, :].astype(F32) * wother[k * T + t, 0:1, :]
            total = mine + theirs if total is None else total + mine + theirs
        return total

    base = 1 + K * groups
    xs, xr, ys, yr, zs, zr = (bufs[kind] for kind in KINDS)

    def step_copy(n, letter):
        s, r = (xs, xr) if letter == "x" else (ys, yr)
        at = base + 2 * n + "xy".index(letter)
        return remote(s[n], r[n], sems_s.at[at], sems_r.at[at], x_dev if letter == "x" else y_dev)

    def line_copy(n, zz):
        return remote(zs[n].at[zz], zr[n].at[z], line_s.at[n, zz], line_r.at[n, z], dev(zz=zz))

    def line_arrival(n, zz):
        return remote(zs[n].at[zz], zr[n].at[zz], line_s.at[n, zz], line_r.at[n, zz], dev(zz=zz))

    def others(f):
        loop(Z - 1, lambda j: f(lax.rem(z + 1 + j, Z)))

    def send(n):
        order = units[n][3]
        if order == "xyz":
            def one(zz):
                for ty in range(2):
                    xs[n][ty, zz] = chip_sum(n, ty, zz, 1 - x).astype(BF16)

            loop(Z, one)
            step_copy(n, "x").start()
        elif order == "yxz":
            def one(zz):
                for xx in range(X):
                    ys[n][zz, xx] = chip_sum(n, 1 - y, zz, xx).astype(BF16)

            loop(Z, one)
            step_copy(n, "y").start()
        else:
            def one(zz):
                for ty in range(2):
                    for xx in range(X):
                        zs[n][zz, ty, xx] = chip_sum(n, ty, zz, xx).astype(BF16)
                line_copy(n, zz).start()

            others(one)

    def line_sum(n, value, pick):
        if Z <= 8:
            for zz in range(Z):
                value = value + pick(zr[n].at[zz])[...].astype(F32)
            return value
        return lax.fori_loop(0, Z, lambda zz, v: v + pick(zr[n].at[zz])[...].astype(F32), value)

    def summed(n, ty, xx):
        return line_sum(n, chip_sum(n, ty, z, xx), lambda ref: ref.at[ty, xx])

    def send_again(n):
        order = units[n][3]
        if order == "xyz":
            step_copy(n, "x").wait_recv()

            def one(zz):
                value = chip_sum(n, 1 - y, zz, x) + xr[n][1 - y, zz].astype(F32)
                ys[n][zz] = value.astype(BF16)

            loop(Z, one)
            step_copy(n, "y").start()
        elif order == "yxz":
            step_copy(n, "y").wait_recv()

            def one(zz):
                value = chip_sum(n, y, zz, 1 - x) + yr[n][zz, 1 - x].astype(F32)
                xs[n][zz] = value.astype(BF16)

            loop(Z, one)
            step_copy(n, "x").start()
        else:
            others(lambda zz: line_arrival(n, zz).wait_recv())
            for j in range(2):
                if order == "zxy":
                    xs[n][j] = summed(n, j, 1 - x).astype(BF16)
                else:
                    ys[n][j] = summed(n, 1 - y, j).astype(BF16)
            step_copy(n, order[1]).start()

    def plane_sum(n, zz):
        value = chip_sum(n, y, zz, x)
        if units[n][3] == "xyz":
            return value + xr[n][y, zz].astype(F32) + yr[n][zz].astype(F32)
        return value + yr[n][zz, x].astype(F32) + xr[n][zz].astype(F32)

    def send_last(n):
        order = units[n][3]
        if order[2] == "z":
            step_copy(n, order[1]).wait_recv()

            def one(zz):
                zs[n][zz] = plane_sum(n, zz).astype(BF16)
                line_copy(n, zz).start()

            others(one)
        elif order == "zxy":
            step_copy(n, "x").wait_recv()
            ys[n][...] = (summed(n, 1 - y, x) + xr[n][1 - y].astype(F32)).astype(BF16)
            step_copy(n, "y").start()
        else:
            step_copy(n, "y").wait_recv()
            xs[n][...] = (summed(n, y, 1 - x) + yr[n][1 - x].astype(F32)).astype(BF16)
            step_copy(n, "x").start()

    def total(n):
        order = units[n][3]
        if order[2] == "z":
            others(lambda zz: line_arrival(n, zz).wait_recv())
            return line_sum(n, plane_sum(n, z), lambda ref: ref)
        step_copy(n, order[2]).wait_recv()
        value = summed(n, y, x)
        if order == "zxy":
            return value + xr[n][y].astype(F32) + yr[n][...].astype(F32)
        return value + yr[n][x].astype(F32) + xr[n][...].astype(F32)

    def final_copy(g):
        at = base + 2 * len(units) + g
        return remote(fsend.at[g], frecv.at[g], sems_s.at[at], sems_r.at[at], c_dev)

    def finish(g):
        at = pl.multiple_of(c * half + g * LANES, LANES)
        for h in range(split):
            span = pl.ds(h * part, part)
            one, two = (total(units.index((g, tc, h, order_of[g, tc, h]))) for tc in range(2))
            out_ref[span, pl.ds(at, LANES)] = jnp.where(c == 0, one, two) * used(at, h * part, part)
            fsend[g, span, :] = jnp.where(c == 0, two, one)
        final_copy(g).start()

    order_of = {unit[:3]: unit[3] for unit in units}
    numbers = [[units.index(unit) for unit in pair] for pair in pairs]
    plain = [pair for i, pair in enumerate(numbers) if i != 1]
    turned = numbers[1]

    def group_of(j):
        return units[plain[j][0]][0]

    def each(f, pair):
        for n in pair:
            f(n)

    ready = set()

    def receive(g):
        if g not in ready:
            ready.add(g)
            for k in range(K):
                core_copy(g, k).wait_recv()

    queue = [(g, k) for g in range(groups) for k in range(K)]

    def compute(count):
        for _ in range(min(count, len(queue))):
            second(*queue.pop(0))

    def compute_to(g):
        while queue and queue[0][0] <= g:
            compute(1)

    steps = len(plain)
    compute(K + 1)
    weights_copy.wait_recv()
    receive(0)
    each(send, plain[0])
    each(send, turned)
    compute_to(group_of(1))
    receive(group_of(1))
    each(send, plain[1])
    compute(K)
    for j in range(steps):
        each(send_again, plain[j])
        if j + 2 < steps:
            compute_to(group_of(j + 2))
            receive(group_of(j + 2))
            each(send, plain[j + 2])
            compute(1)
        if j == steps - 1:
            each(send_again, turned)
        if j >= 1:
            each(send_last, plain[j - 1])
    each(send_last, plain[steps - 1])
    each(send_last, turned)
    for g in (*range(1, groups - 1), 0, groups - 1):
        finish(g)
    for g in range(groups):
        final_copy(g).wait_recv()
        at = pl.multiple_of((1 - c) * half + g * LANES, LANES)
        out_ref[:, pl.ds(at, LANES)] = frecv[g] * used(at)

    def drain(q):
        for p in range(pieces):
            @pl.when(jnp.logical_and(has_up, q <= z))
            def _():
                hop(q, 0, p).wait_send()

            @pl.when(jnp.logical_and(has_dn, q >= z))
            def _():
                hop(q, 1, p).wait_send()

            @pl.when(jnp.logical_not(skips_x(q, p)))
            def _():
                hop(q, 2, p).wait_send()

    loop(Z, drain)
    relays(lambda copy: copy.wait_send())
    weights_copy.wait_send()
    for g in range(groups):
        final_copy(g).wait_send()
        for k in range(K):
            core_copy(g, k).wait_send()
    for n in range(len(units)):
        step_copy(n, "x").wait_send()
        step_copy(n, "y").wait_send()
        others(lambda zz, n=n: line_copy(n, zz).wait_send())


def kernel_entry(cfg, *refs):
    count = len([unit for pair in cfg[8] for unit in pair])
    plain, rest = refs[:21], refs[21:]
    bufs = {kind: rest[i * count : (i + 1) * count] for i, kind in enumerate(KINDS)}
    step_kernel(cfg, *plain, *rest[len(KINDS) * count :], bufs)


def unit_shapes(order, Z, X, tail):
    lead = {
        "xyz": ((2, Z), (Z,), (Z,)),
        "yxz": ((Z,), (Z, X), (Z,)),
        "zxy": ((2,), (), (Z, 2, X)),
        "zyx": ((), (X,), (Z, 2, X)),
    }[order]
    return [pltpu.VMEM(shape + tail, BF16) for shape in lead]


def body(wave, left_ops, right_ops, targets, sector_sizes, pair_ids, pair_coefficients):
    block = wave.shape[2]
    rows = wave.shape[1]
    K = left_ops.shape[0]
    T = sector_sizes.shape[0]
    pairs = lax.axis_size("pair")
    X = 2
    Z = pairs // X
    half = block // 2
    groups = half // LANES
    split = 2 if rows % 32 == 0 else 1
    unit_pairs = plan(groups, split)
    units = [unit for pair in unit_pairs for unit in pair]
    shapes = [unit_shapes(unit[3], Z, X, (rows // split, LANES)) for unit in units]
    unit_bufs = [shape[axis] for axis in range(3) for _ in range(2) for shape in shapes]
    count = 1 + K * groups + 2 * len(units) + groups
    dma = pltpu.SemaphoreType.DMA
    cfg = (Z, X, T, K, rows, block, groups, split, unit_pairs)
    planewise = (X * rows) % PLANE_DEPTH == 0
    vmem, hbm = pl.BlockSpec(memory_space=pltpu.VMEM), pl.BlockSpec(memory_space=pltpu.HBM)
    smem = pl.BlockSpec(memory_space=pltpu.SMEM)
    operands = (
        wave[0], targets.reshape(-1), sector_sizes, pair_ids, pair_coefficients, left_ops[:, 0], right_ops[:, 0]
    )
    out = pl.pallas_call(
        functools.partial(kernel_entry, cfg),
        out_shape=jax.ShapeDtypeStruct((rows, block), F32),
        in_specs=[hbm, smem, smem, smem, smem, hbm, hbm],
        out_specs=vmem,
        scratch_shapes=[
            pltpu.VMEM((rows, block), BF16),
            pltpu.VMEM((Z, X, rows, block), BF16),
            pltpu.VMEM((K, block, block), BF16),
            pltpu.VMEM((K, groups, 2, LANES, block), BF16),
            pltpu.VMEM((K, block, block) if planewise else (8, LANES), F32),
            pltpu.VMEM((K, block, block), BF16),
            pltpu.VMEM((groups, K, block, LANES), F32),
            pltpu.VMEM((groups, K, block, LANES), BF16),
            pltpu.VMEM((groups, K, block, LANES), BF16),
            pltpu.VMEM((K * T, 8, LANES), F32),
            pltpu.VMEM((K * T, 8, LANES), F32),
            pltpu.VMEM((groups, rows, LANES), F32),
            pltpu.VMEM((groups, rows, LANES), F32),
            *unit_bufs,
            dma((K + 1 + 2 * K * groups,)), dma((count,)), dma((count,)),
            dma((len(units), Z)), dma((len(units), Z)), dma((3, Z, PIECES)), dma((Z, X, PIECES)), dma((2,)),
        ],
        compiler_params=pltpu.CompilerParams(
            collective_id=0, has_side_effects=True, vmem_limit_bytes=VMEM_LIMIT
        ),
        name="sigma_step",
    )(*(pltpu.with_memory_space_constraint(a, pltpu.HBM) for a in operands))
    return out[None]


def solution(mesh):
    placed = (
        P("sector", "pair", None),
        P("pair", "sector", None, None),
        P("pair", "sector", None, None),
        P("pair", "sector"),
        P(),
        P("pair"),
        P(),
    )
    return jax.shard_map(
        body, mesh=mesh, in_specs=placed, out_specs=P("sector", "pair", None), check_vma=False
    )
```

time: 93.4 us -> 78.8 us (0.84)
  Pallas kernels: 86.4 us -> 77.9 us
  local copies, waits for them, and re-layouts: 6.55 us -> 0.8 us
    pallas_call x1, Pallas kernels: 86.4 us -> 77.9 us  [body(): pl.pallas_call(functools.partial(kernel_entry, cfg), out_shape=jax.ShapeD...]
    unnamed x13 -> x1, local copies, waits for them, and re-layouts: 6.55 us -> 0.8 us
where the time goes in v2:
time: 78.8 us; the launch traced here: 78.7 us
  Pallas kernels  77.9 us (99%)
  local copies, waits for them, and re-layouts  0.8 us (1%)
    pallas_call x1, Pallas kernels, body(): pl.pallas_call(functools.partial(kernel_entry, cfg), out_shape=jax.ShapeD...  77.9 us

profile of v2, /device:TPU:0, one launch (start us, length us, event | category | flops | bytes accessed | tf_op | source)
XLA Modules:
  0.0 78.7 jit_solution(6247536832318686196)
XLA Ops:
  0.0 77.9 %sigma_step.1 = f32[128,1024]{1,0:T(8,128)S(1)} custom-call(bf16[128,1024]{1,0:T(8,128)(2,1)} %bitcast.8, s32[2]{0:T(128)} %bitcast.9, s32[4]{0:T(128)} %refs_2_.1, s32[2]{0:T(128)} %refs_3_.1, f32[16]{0:T(128)} %refs_4_.1, bf16[2,1024,1024]{2,1,0:T(8,128)(2,1)} %bitcast.6, bf16[2,1024,1024]{2,1,0:T(8,128)(2,1)} %bitcast.7), custom_call_target="tpu_custom_call" | custom-call | tf_op jit(solution)/shard_map/sigma_step/pallas_call | solution.py:549
  77.9 0.8 %copy.9 = f32[1,128,1024]{2,1,0:T(8,128)} copy(f32[1,128,1024]{2,1,0:T(8,128)S(1)} %bitcast.5) | data formatting | bytes 1048576

commit v3 on v2

v3 whole, which is shorter than its diff:
```python
import functools

import jax
import jax.numpy as jnp
from jax import lax
from jax.experimental import pallas as pl
from jax.experimental.pallas import tpu as pltpu
from jax.sharding import PartitionSpec as P

MESH = pl.DeviceIdType.MESH
F32 = jnp.float32
BF16 = jnp.bfloat16
LANES = 128
PLANE_DEPTH = 128
ROW_TILE = 512
PIECES = 2
VMEM_LIMIT = 48 * 1024 * 1024


class Unit:
    def __init__(self, group, core, start, count, order):
        self.group, self.core, self.start, self.count, self.order = group, core, start, count, order


def plan(groups, rows):
    pairs = []
    for g in range(groups):
        parts = 1 if rows % 32 else 4 if g == groups - 1 and rows % 64 == 0 else 2
        count = rows // parts
        if parts == 1:
            found = [[(g, tc, 0, rows) for tc in range(2)]]
        else:
            found = [
                [(g, tc, (i + h) * count, count) for h in range(2)] for tc in range(2) for i in range(0, parts, 2)
            ]
        pairs += found
    orders = [("zxy", "zyx") if n == 1 else ("xyz", "yxz") for n in range(len(pairs))]
    return [[Unit(*part, order) for part, order in zip(pair, way)] for pair, way in zip(pairs, orders)]


def unit_sizes(unit, Z, X):
    return {
        "xyz": (2 * Z, Z, Z),
        "yxz": (Z, Z * X, Z),
        "zxy": (2, 1, Z * 2 * X),
        "zyx": (1, X, Z * 2 * X),
    }[unit.order]


def step_kernel(
    cfg, wave_hbm, targets_hbm, sizes_hbm, ids_hbm, coefs_hbm, left_hbm, right_hbm, out_ref,
    targets_ref, sizes_ref, ids_ref, coefs_ref,
    wave_ref, wbuf, lbuf, rbuf, acc, left, own, psend, precv, weight_ref, wother, fsend, frecv,
    xs, xr, ys, yr, zs, zr, load_sem, send_sem, recv_sem, pair_sem, gat_s, gat_r, relay_s,
):
    Z, X, T, K, rows, block, groups, pairs = cfg
    units = [unit for pair in pairs for unit in pair]
    offsets, ends = [], [0, 0, 0]
    for unit in units:
        offsets.append(tuple(ends))
        ends = [end + size * unit.count for end, size in zip(ends, unit_sizes(unit, Z, X))]
    half = block // 2
    pair, sector = lax.axis_index("pair"), lax.axis_index("sector")
    z, x = pair // X, lax.rem(pair, X)
    y, c = sector // 2, lax.rem(sector, 2)

    def dev(zz=None, xx=None, yy=None, cc=None):
        zz, xx = z if zz is None else zz, x if xx is None else xx
        yy, cc = y if yy is None else yy, c if cc is None else cc
        return (zz * X + xx, yy * 2 + cc)

    x_dev, y_dev, c_dev = dev(xx=1 - x), dev(yy=1 - y), dev(cc=1 - c)
    up_dev, dn_dev = dev(zz=z + 1), dev(zz=z - 1)

    def loop(count, f):
        def one(i, carry):
            f(i)
            return carry

        lax.fori_loop(0, count, one, 0)

    has_up, has_dn = z + 1 < Z, z >= 1

    left_loads = [pltpu.make_async_copy(left_hbm.at[k], lbuf.at[k], load_sem.at[0]) for k in range(K)]
    right_loads = []
    for k in range(K):
        for g in range(groups):
            for j in range(2):
                at = pl.multiple_of((1 - c if j == 0 else c) * half + g * LANES, LANES)
                right_loads.append(
                    pltpu.make_async_copy(
                        right_hbm.at[k, pl.ds(at, LANES)], rbuf.at[k, g, j],
                        load_sem.at[1],
                    )
                )

    barrier = pltpu.get_barrier_semaphore()
    for other in (x_dev, y_dev, c_dev):
        pl.semaphore_signal(barrier, inc=1, device_id=other, device_id_type=MESH)

    wave_load = pltpu.make_async_copy(wave_hbm, wave_ref, load_sem.at[2])
    wave_load.start()
    small_loads = [
        pltpu.make_async_copy(src, dst, load_sem.at[3 + i])
        for i, (src, dst) in enumerate(
            ((targets_hbm, targets_ref), (sizes_hbm, sizes_ref), (ids_hbm, ids_ref), (coefs_hbm, coefs_ref))
        )
    ]
    for copy in small_loads:
        copy.start()

    @pl.when(has_up)
    def _():
        pl.semaphore_signal(barrier, inc=1, device_id=up_dev, device_id_type=MESH)

    @pl.when(has_dn)
    def _():
        pl.semaphore_signal(barrier, inc=1, device_id=dn_dev, device_id_type=MESH)

    def rows_of(n, axis, index):
        count = units[n].count
        return pl.ds(pl.multiple_of(offsets[n][axis] + index * count, count), count)

    def z_index(n, zz, ty=0, xx=0):
        return zz if units[n].order[2] == "z" else (zz * 2 + ty) * X + xx

    for n, unit in enumerate(units):
        size = unit_sizes(unit, Z, X)[2] // Z * unit.count
        zr[pl.ds(pl.multiple_of(offsets[n][2] + z * size, unit.count), size), :] = jnp.zeros((size, LANES), BF16)
    for copy in left_loads:
        copy.start()
    for copy in small_loads:
        copy.wait()
    for k in range(K):
        factor = coefs_ref[ids_ref[k]]
        for t in range(T):
            chosen = jnp.where(targets_ref[k] == t, factor, 0.0)
            weight_ref[k * T + t] = jnp.full((8, LANES), chosen, F32)
    size = sizes_ref[sector]

    def used(column, start=0, count=rows):
        row_ids = pair * rows + start + lax.broadcasted_iota(jnp.int32, (count, LANES), 0)
        lane_ids = column + lax.broadcasted_iota(jnp.int32, (count, LANES), 1)
        return ((row_ids < size) & (lane_ids < size)).astype(F32)

    wave_load.wait()
    for at in range(0, block, LANES):
        value = wave_ref[:, at : at + LANES].astype(F32) * used(at)
        wbuf[z, x, :, at : at + LANES] = value.astype(jnp.bfloat16)
    pl.semaphore_wait(barrier, 3 + has_up.astype(jnp.int32) + has_dn.astype(jnp.int32))

    def remote(src, dst, ss, rs, device):
        return pltpu.make_async_remote_copy(
            src_ref=src, dst_ref=dst, send_sem=ss, recv_sem=rs, device_id=device, device_id_type=MESH
        )

    piece = rows // PIECES if rows % (16 * PIECES) == 0 else rows
    pieces = rows // piece

    def block_at(q, xx, p):
        return wbuf.at[q, xx, pl.ds(p * piece, piece)]

    def hop(q, way, p):
        device = (up_dev, dn_dev, x_dev)[way]
        return remote(block_at(q, x, p), block_at(q, x, p), gat_s.at[way], gat_r.at[q, x, p], device)

    def arrival(q, xx, p):
        return remote(block_at(q, xx, p), block_at(q, xx, p), gat_s.at[2], gat_r.at[q, xx, p], x_dev)

    relayed = Z >= 3 and pieces >= 2
    last = pieces - 1

    def skips_x(q, p):
        if not relayed or p != last:
            return jnp.bool_(False)
        source = jnp.where(z == 0, 1, jnp.where(z == Z - 1, Z - 2, jnp.where(z < Z // 2, z - 1, z + 1)))
        return q == source

    def relay(way):
        device = (up_dev, dn_dev)[way]
        block_there = block_at(z, 1 - x, last)
        return remote(block_there, block_there, relay_s.at[way], gat_r.at[z, 1 - x, last], device)

    def relays_to_ends(f):
        if relayed:
            @pl.when(z == Z - 2)
            def _():
                f(relay(0))

            @pl.when(z == 1)
            def _():
                f(relay(1))

    def relays_inward(f):
        if relayed:
            @pl.when(z + 1 < Z // 2)
            def _():
                f(relay(0))

            @pl.when((z - 1 >= Z // 2) & (z >= 1))
            def _():
                f(relay(1))

    def pass_on(q, ways, p):
        if 0 in ways:
            @pl.when(has_up)
            def _():
                hop(q, 0, p).start()

        if 1 in ways:
            @pl.when(has_dn)
            def _():
                hop(q, 1, p).start()

        @pl.when(jnp.logical_not(skips_x(q, p)))
        def _():
            hop(q, 2, p).start()

    for p in range(pieces):
        pass_on(z, (0, 1), p)
    weights_copy = remote(weight_ref, wother, send_sem.at[0], recv_sem.at[0], c_dev)
    weights_copy.start()
    for copy in right_loads:
        copy.start()

    depth = X * rows
    planewise = depth % PLANE_DEPTH == 0
    tile = min(ROW_TILE, block)
    tiles = block // tile

    def multiply(q, stage):
        plane = wbuf.at[q]

        def one(i, carry):
            k, at = i // tiles, pl.multiple_of(lax.rem(i, tiles) * tile, tile)
            cols = pl.ds(pl.multiple_of(q * depth, depth), depth)
            product = jnp.dot(
                lbuf[k, pl.ds(at, tile), cols], plane[...].reshape(depth, block), preferred_element_type=F32
            )
            if stage == "only":
                left[k, pl.ds(at, tile), :] = product.astype(BF16)
            elif stage == "first":
                acc[k, pl.ds(at, tile), :] = product
            elif stage == "middle":
                acc[k, pl.ds(at, tile), :] += product
            else:
                left[k, pl.ds(at, tile), :] = (acc[k, pl.ds(at, tile), :] + product).astype(BF16)
            return carry

        lax.fori_loop(0, K * tiles, one, 0)

    def take_plane(q, stage):
        for p in range(pieces):
            arrival(q, 1 - x, p).wait_recv()
        if stage == "first":
            relays_inward(lambda copy: copy.start())
        if planewise:
            multiply(q, stage)

    pltpu.make_async_copy(lbuf, lbuf, load_sem.at[0]).wait()

    def forward(d, carry):
        lo, hi = z - d, z + d
        for p in range(pieces):
            @pl.when(lo >= 0)
            def _():
                arrival(lo, x, p).wait_recv()
                pass_on(lo, (0,), p)

            @pl.when(hi < Z)
            def _():
                arrival(hi, x, p).wait_recv()
                pass_on(hi, (1,), p)

        @pl.when(d == 1)
        def _():
            take_plane(z, "first")

        return carry

    if Z == 1:
        take_plane(z, "only")
    lax.fori_loop(1, Z, forward, 0)
    relays_to_ends(lambda copy: copy.start())
    near = jnp.minimum(z, Z - 1 - z)

    def plane_by_distance(i):
        d = (i + 1) // 2
        both = jnp.where(lax.rem(i, 2) == 1, z - d, z + d)
        return jnp.where(i <= 2 * near, both, jnp.where(z > near, z - (i - near), z + (i - near)))

    def take_planes(i, carry):
        take_plane(plane_by_distance(i), "middle")
        return carry

    lax.fori_loop(1, Z - 1, take_planes, 0)
    if Z > 1:
        take_plane(plane_by_distance(jnp.int32(Z - 1)), "last")

    def whole_left(i, carry):
        k, at = i // tiles, pl.multiple_of(lax.rem(i, tiles) * tile, tile)
        value = jnp.dot(
            lbuf[k, pl.ds(at, tile), :], wbuf[...].reshape(block, block), preferred_element_type=F32
        )
        left[k, pl.ds(at, tile), :] = value.astype(BF16)
        return carry

    if not planewise:
        lax.fori_loop(0, K * tiles, whole_left, 0)
    pltpu.make_async_copy(rbuf, rbuf, load_sem.at[1]).wait()

    def core_copy(g, k):
        return remote(psend.at[g, k], precv.at[g, k], send_sem.at[1], recv_sem.at[1 + g], c_dev)

    def core_arrival(g):
        return remote(psend.at[g], precv.at[g], send_sem.at[1], recv_sem.at[1 + g], c_dev)

    def second(g, k):
        def one(i, carry):
            at = pl.multiple_of(i * tile, tile)
            term = lax.dot_general(
                left[k, pl.ds(at, tile), :], rbuf[k, g].reshape(2 * LANES, block),
                (((1,), (1,)), ((), ())), preferred_element_type=F32,
            )
            psend[g, k, pl.ds(at, tile), :] = term[:, :LANES].astype(BF16)
            own[g, k, pl.ds(at, tile), :] = term[:, LANES:]
            return carry

        lax.fori_loop(0, tiles, one, 0)
        core_copy(g, k).start()

    def chip_sum(n, ty, zz, xx):
        unit = units[n]
        at = pl.ds(pl.multiple_of((zz * X + xx) * rows + unit.start, unit.count), unit.count)
        t = ty * 2 + unit.core
        total = None
        for k in range(K):
            mine = own[unit.group, k, at, :] * weight_ref[k * T + t, 0:1, :]
            theirs = precv[unit.group, k, at, :].astype(F32) * wother[k * T + t, 0:1, :]
            total = mine + theirs if total is None else total + mine + theirs
        return total

    def put_x(n, index, value):
        xs[rows_of(n, 0, index), :] = value.astype(BF16)

    def put_y(n, index, value):
        ys[rows_of(n, 1, index), :] = value.astype(BF16)

    def put_z(n, index, value):
        zs[rows_of(n, 2, index), :] = value.astype(BF16)

    def from_x(n, index):
        return xr[rows_of(n, 0, index), :].astype(F32)

    def from_y(n, index):
        return yr[rows_of(n, 1, index), :].astype(F32)

    def from_z(n, index):
        return zr[rows_of(n, 2, index), :].astype(F32)

    def step_copy(n, letter, slot):
        axis = "xy".index(letter)
        s, r = ((xs, xr), (ys, yr))[axis]
        span = pl.ds(offsets[n][axis], unit_sizes(units[n], Z, X)[axis] * units[n].count)
        device = (x_dev, y_dev)[axis]
        return remote(s.at[span], r.at[span], send_sem.at[2 + axis], pair_sem.at[pair_of[n], slot], device)

    def z_span(n, zz):
        size = unit_sizes(units[n], Z, X)[2] // Z * units[n].count
        return pl.ds(pl.multiple_of(offsets[n][2] + zz * size, units[n].count), size)

    def line_slot(n):
        return 2 if units[n].order[2] == "z" else 0

    def line_copy(n, zz):
        sem = pair_sem.at[pair_of[n], line_slot(n)]
        return remote(zs.at[z_span(n, zz)], zr.at[z_span(n, z)], send_sem.at[4], sem, dev(zz=zz))

    def wait_rows(sem, count):
        if count:
            pltpu.make_async_copy(zs.at[pl.ds(0, count)], zs.at[pl.ds(0, count)], sem).wait()

    def wait_pair(i, slot):
        count = 0
        for n in numbers[i]:
            unit, sizes = units[n], unit_sizes(units[n], Z, X)
            letter = unit.order[slot]
            count += (sizes["xyz".index(letter)] // Z * (Z - 1) if letter == "z" else sizes["xyz".index(letter)]) * unit.count
        wait_rows(pair_sem.at[i, slot], count)

    def others(f):
        loop(Z - 1, lambda j: f(lax.rem(z + 1 + j, Z)))

    def send(n):
        order = units[n].order
        if order == "xyz":
            def one(zz):
                for ty in range(2):
                    put_x(n, ty * Z + zz, chip_sum(n, ty, zz, 1 - x))

            loop(Z, one)
            step_copy(n, "x", 0).start()
        elif order == "yxz":
            def one(zz):
                for xx in range(X):
                    put_y(n, zz * X + xx, chip_sum(n, 1 - y, zz, xx))

            loop(Z, one)
            step_copy(n, "y", 0).start()
        else:
            def one(zz):
                for ty in range(2):
                    for xx in range(X):
                        put_z(n, z_index(n, zz, ty, xx), chip_sum(n, ty, zz, xx))
                line_copy(n, zz).start()

            others(one)

    def line_sum(n, value, ty=0, xx=0):
        if Z <= 8:
            for zz in range(Z):
                value = value + from_z(n, z_index(n, zz, ty, xx))
            return value
        return lax.fori_loop(0, Z, lambda zz, v: v + from_z(n, z_index(n, zz, ty, xx)), value)

    def summed(n, ty, xx):
        return line_sum(n, chip_sum(n, ty, z, xx), ty, xx)

    def send_again(n):
        order = units[n].order
        if order == "xyz":
            def one(zz):
                put_y(n, zz, chip_sum(n, 1 - y, zz, x) + from_x(n, (1 - y) * Z + zz))

            loop(Z, one)
        elif order == "yxz":
            def one(zz):
                put_x(n, zz, chip_sum(n, y, zz, 1 - x) + from_y(n, zz * X + 1 - x))

            loop(Z, one)
        else:
            for j in range(2):
                if order == "zxy":
                    put_x(n, j, summed(n, j, 1 - x))
                else:
                    put_y(n, j, summed(n, 1 - y, j))
        step_copy(n, order[1], 1).start()

    def plane_sum(n, zz):
        value = chip_sum(n, y, zz, x)
        if units[n].order == "xyz":
            return value + from_x(n, y * Z + zz) + from_y(n, zz)
        return value + from_y(n, zz * X + x) + from_x(n, zz)

    def send_last(n):
        order = units[n].order
        if order[2] == "z":
            def one(zz):
                put_z(n, zz, plane_sum(n, zz))
                line_copy(n, zz).start()

            others(one)
        elif order == "zxy":
            put_y(n, 0, summed(n, 1 - y, x) + from_x(n, 1 - y))
            step_copy(n, "y", 2).start()
        else:
            put_x(n, 0, summed(n, y, 1 - x) + from_y(n, 1 - x))
            step_copy(n, "x", 2).start()

    def total(n):
        order = units[n].order
        if order[2] == "z":
            return line_sum(n, plane_sum(n, z))
        if order == "zxy":
            return summed(n, y, x) + from_x(n, y) + from_y(n, 0)
        return summed(n, y, x) + from_y(n, x) + from_x(n, 0)

    def final_copy(g):
        return remote(fsend.at[g], frecv.at[g], send_sem.at[5], recv_sem.at[1 + groups + g], c_dev)

    numbers, pair_of = [], {}
    for i, members in enumerate(pairs):
        numbers.append([units.index(unit) for unit in members])
        for n in numbers[i]:
            pair_of[n] = i

    def finish(g):
        at = pl.multiple_of(c * half + g * LANES, LANES)
        for i in range(len(pairs)):
            if units[numbers[i][0]].group == g:
                wait_pair(i, 2)
        here = [n for n in range(len(units)) if units[n].group == g]
        for n in here:
            if units[n].core == 0:
                start, count = units[n].start, units[n].count
                twin = [m for m in here if units[m].core == 1 and units[m].start == start]
                one, two = total(n), total(twin[0])
                span = pl.ds(start, count)
                out_ref[span, pl.ds(at, LANES)] = jnp.where(c == 0, one, two) * used(at, start, count)
                fsend[g, span, :] = jnp.where(c == 0, two, one)
        final_copy(g).start()

    def each(f, i):
        for n in numbers[i]:
            f(n)

    ready = set()

    def receive(g):
        if g not in ready:
            ready.add(g)
            core_arrival(g).wait_recv()

    queue = [(g, k) for g in range(groups) for k in range(K)]

    def compute(count):
        for _ in range(min(count, len(queue))):
            second(*queue.pop(0))

    def start_pair(i):
        g = units[numbers[i][0]].group
        while queue and queue[0][0] <= g:
            compute(1)
        receive(g)
        each(send, i)

    turned = 1
    plain = [i for i in range(len(pairs)) if i != turned]
    steps = len(plain)
    done = set()
    compute(K + 1)
    weights_copy.wait_recv()
    start_pair(plain[0])
    start_pair(turned)
    start_pair(plain[1])
    compute(K)
    for j in range(steps):
        wait_pair(plain[j], 0)
        each(send_again, plain[j])
        if j + 2 < steps:
            start_pair(plain[j + 2])
            compute(1)
        if j == max(0, steps - 3):
            wait_pair(turned, 0)
            each(send_again, turned)
        if j == steps - 1:
            wait_pair(turned, 1)
            each(send_last, turned)
        if j >= 1:
            wait_pair(plain[j - 1], 1)
            each(send_last, plain[j - 1])
        if j >= steps - 2 and 1 + j - (steps - 2) < groups - 1:
            finish(1 + j - (steps - 2))
            done.add(1 + j - (steps - 2))
    wait_pair(plain[steps - 1], 1)
    each(send_last, plain[steps - 1])
    for g in (*range(1, groups - 1), 0, groups - 1):
        if g not in done:
            done.add(g)
            finish(g)
    for g in range(groups):
        final_copy(g).wait_recv()
        at = pl.multiple_of((1 - c) * half + g * LANES, LANES)
        out_ref[:, pl.ds(at, LANES)] = frecv[g] * used(at)

    for v in range(Z):
        @pl.when(z == v)
        def _(v=v):
            for way, count in ((0, v + 1 if v + 1 < Z else 0), (1, Z - v if v else 0)):
                if count:
                    span = wbuf.at[pl.ds(0, count), 0]
                    pltpu.make_async_copy(span, span, gat_s.at[way]).wait()

    count = Z * rows - (piece if relayed else 0)
    flat = left.at[0, pl.ds(0, count)]
    pltpu.make_async_copy(flat, flat, gat_s.at[2]).wait()
    relays_to_ends(lambda copy: copy.wait_send())
    relays_inward(lambda copy: copy.wait_send())
    weights_copy.wait_send()
    pltpu.make_async_copy(psend, psend, send_sem.at[1]).wait()
    pltpu.make_async_copy(xs, xs, send_sem.at[2]).wait()
    pltpu.make_async_copy(ys, ys, send_sem.at[3]).wait()
    wait_rows(send_sem.at[4], zs.shape[0] // Z * (Z - 1))
    pltpu.make_async_copy(fsend, fsend, send_sem.at[5]).wait()


def body(wave, left_ops, right_ops, targets, sector_sizes, pair_ids, pair_coefficients):
    block = wave.shape[2]
    rows = wave.shape[1]
    K = left_ops.shape[0]
    T = sector_sizes.shape[0]
    X = 2
    Z = lax.axis_size("pair") // X
    groups = block // 2 // LANES
    pairs = plan(groups, rows)
    heights = [0, 0, 0]
    for pair in pairs:
        for unit in pair:
            heights = [height + size * unit.count for height, size in zip(heights, unit_sizes(unit, Z, X))]
    dma = pltpu.SemaphoreType.DMA
    planewise = (X * rows) % PLANE_DEPTH == 0
    hbm = pl.BlockSpec(memory_space=pltpu.HBM)
    operands = (
        wave[0], targets.reshape(-1), sector_sizes, pair_ids, pair_coefficients, left_ops[:, 0], right_ops[:, 0]
    )
    out = pl.pallas_call(
        functools.partial(step_kernel, (Z, X, T, K, rows, block, groups, pairs)),
        out_shape=jax.ShapeDtypeStruct((rows, block), F32),
        in_specs=[hbm] * 7,
        out_specs=pl.BlockSpec(memory_space=pltpu.VMEM),
        scratch_shapes=[
            *(pltpu.SMEM(a.shape, a.dtype) for a in operands[1:5]),
            pltpu.VMEM((rows, block), BF16),
            pltpu.VMEM((Z, X, rows, block), BF16),
            pltpu.VMEM((K, block, block), BF16),
            pltpu.VMEM((K, groups, 2, LANES, block), BF16),
            pltpu.VMEM((K, block, block) if planewise else (8, LANES), F32),
            pltpu.VMEM((K, block, block), BF16),
            pltpu.VMEM((groups, K, block, LANES), F32),
            pltpu.VMEM((groups, K, block, LANES), BF16),
            pltpu.VMEM((groups, K, block, LANES), BF16),
            pltpu.VMEM((K * T, 8, LANES), F32),
            pltpu.VMEM((K * T, 8, LANES), F32),
            pltpu.VMEM((groups, rows, LANES), F32),
            pltpu.VMEM((groups, rows, LANES), F32),
            *(pltpu.VMEM((height, LANES), BF16) for height in heights for _ in range(2)),
            dma((7,)), dma((6,)), dma((1 + 2 * groups,)), dma((len(pairs), 3)),
            dma((3,)), dma((Z, X, PIECES)), dma((2,)),
        ],
        compiler_params=pltpu.CompilerParams(
            collective_id=0, has_side_effects=True, vmem_limit_bytes=VMEM_LIMIT
        ),
        name="sigma_step",
    )(*(pltpu.with_memory_space_constraint(a, pltpu.HBM) for a in operands))
    return out[None]


def solution(mesh):
    placed = (
        P("sector", "pair", None),
        P("pair", "sector", None, None),
        P("pair", "sector", None, None),
        P("pair", "sector"),
        P(),
        P("pair"),
        P(),
    )
    return jax.shard_map(
        body, mesh=mesh, in_specs=placed, out_specs=P("sector", "pair", None), check_vma=False
    )
```

time: 78.8 us -> 75.2 us (0.954)
  Pallas kernels: 77.9 us -> 74.3 us
    pallas_call x1, Pallas kernels: 77.9 us -> 74.3 us  [body(): pl.pallas_call(functools.partial(step_kernel, (Z, X, T, K, rows, block, g...]
where the time goes in v3:
time: 75.2 us; the launch traced here: 75.1 us
  Pallas kernels  74.3 us (99%)
  local copies, waits for them, and re-layouts  0.8 us (1%)
    pallas_call x1, Pallas kernels, body(): pl.pallas_call(functools.partial(step_kernel, (Z, X, T, K, rows, block, g...  74.3 us

profile of v3, /device:TPU:0, one launch (start us, length us, event | category | flops | bytes accessed | tf_op | source)
XLA Modules:
  0.0 75.1 jit_solution(428653787423190725)
XLA Ops:
  0.0 74.3 %sigma_step.1 = f32[128,1024]{1,0:T(8,128)S(1)} custom-call(bf16[128,1024]{1,0:T(8,128)(2,1)} %bitcast.8, s32[2]{0:T(128)} %bitcast.9, s32[4]{0:T(128)} %sizes_hbm.1, s32[2]{0:T(128)} %ids_hbm.1, f32[16]{0:T(128)} %coefs_hbm.1, bf16[2,1024,1024]{2,1,0:T(8,128)(2,1)} %bitcast.6, bf16[2,1024,1024]{2,1,0:T(8,128)(2,1)} %bitcast.7), custom_call_target="tpu_custom_call" | custom-call | tf_op jit(solution)/shard_map/sigma_step/pallas_call | solution.py:606
  74.3 0.8 %copy.9 = f32[1,128,1024]{2,1,0:T(8,128)} copy(f32[1,128,1024]{2,1,0:T(8,128)S(1)} %bitcast.5) | data formatting | bytes 1048576

commit v4 on v3

--- a/solution.py
+++ b/solution.py
@@ -11,9 +11,8 @@
 F32 = jnp.float32
 BF16 = jnp.bfloat16
 LANES = 128
-PLANE_DEPTH = 128
-ROW_TILE = 512
-PIECES = 2
+ROW_TILE = 1024
+PIECES = 4
 VMEM_LIMIT = 48 * 1024 * 1024
 
 
@@ -50,7 +49,7 @@
 def step_kernel(
     cfg, wave_hbm, targets_hbm, sizes_hbm, ids_hbm, coefs_hbm, left_hbm, right_hbm, out_ref,
     targets_ref, sizes_ref, ids_ref, coefs_ref,
-    wave_ref, wbuf, lbuf, rbuf, acc, left, own, psend, precv, weight_ref, wother, fsend, frecv,
+    wave_ref, wbuf, lbuf, rbuf, acc, first_acc, left, own, psend, precv, weight_ref, wother, fsend, frecv,
     xs, xr, ys, yr, zs, zr, load_sem, send_sem, recv_sem, pair_sem, gat_s, gat_r, relay_s,
 ):
     Z, X, T, K, rows, block, groups, pairs = cfg
@@ -80,6 +79,10 @@
         lax.fori_loop(0, count, one, 0)
 
     has_up, has_dn = z + 1 < Z, z >= 1
+    nested = Z == 4 and rows % LANES == 0
+    pieces = PIECES
+    width = block // pieces
+    late = range(pieces // 2, pieces) if nested else ()
 
     left_loads = [pltpu.make_async_copy(left_hbm.at[k], lbuf.at[k], load_sem.at[0]) for k in range(K)]
     right_loads = []
@@ -146,7 +149,9 @@
     wave_load.wait()
     for at in range(0, block, LANES):
         value = wave_ref[:, at : at + LANES].astype(F32) * used(at)
-        wbuf[z, x, :, at : at + LANES] = value.astype(jnp.bfloat16)
+        p = at // width
+        where = (x, p, z) if nested else (p, z, x)
+        wbuf[(*where, slice(None), slice(at - p * width, at - p * width + LANES))] = value.astype(BF16)
     pl.semaphore_wait(barrier, 3 + has_up.astype(jnp.int32) + has_dn.astype(jnp.int32))
 
     def remote(src, dst, ss, rs, device):
@@ -154,11 +159,8 @@
             src_ref=src, dst_ref=dst, send_sem=ss, recv_sem=rs, device_id=device, device_id_type=MESH
         )
 
-    piece = rows // PIECES if rows % (16 * PIECES) == 0 else rows
-    pieces = rows // piece
-
     def block_at(q, xx, p):
-        return wbuf.at[q, xx, pl.ds(p * piece, piece)]
+        return wbuf.at[(xx, p, q) if nested else (p, q, xx)]
 
     def hop(q, way, p):
         device = (up_dev, dn_dev, x_dev)[way]
@@ -167,39 +169,20 @@
     def arrival(q, xx, p):
         return remote(block_at(q, xx, p), block_at(q, xx, p), gat_s.at[2], gat_r.at[q, xx, p], x_dev)
 
-    relayed = Z >= 3 and pieces >= 2
-    last = pieces - 1
-
     def skips_x(q, p):
-        if not relayed or p != last:
+        if p not in late:
             return jnp.bool_(False)
-        source = jnp.where(z == 0, 1, jnp.where(z == Z - 1, Z - 2, jnp.where(z < Z // 2, z - 1, z + 1)))
-        return q == source
-
-    def relay(way):
-        device = (up_dev, dn_dev)[way]
-        block_there = block_at(z, 1 - x, last)
-        return remote(block_there, block_there, relay_s.at[way], gat_r.at[z, 1 - x, last], device)
-
-    def relays_to_ends(f):
-        if relayed:
-            @pl.when(z == Z - 2)
-            def _():
-                f(relay(0))
-
-            @pl.when(z == 1)
-            def _():
-                f(relay(1))
-
-    def relays_inward(f):
-        if relayed:
-            @pl.when(z + 1 < Z // 2)
-            def _():
-                f(relay(0))
-
-            @pl.when((z - 1 >= Z // 2) & (z >= 1))
-            def _():
-                f(relay(1))
+        return q == jnp.where(z == 0, 2, jnp.where(z == 1, 0, jnp.where(z == 2, 3, 1)))
+
+    def relay(q, way):
+        for p in late:
+            block_there = block_at(q, 1 - x, p)
+            remote(block_there, block_there, relay_s.at[0], gat_r.at[q, 1 - x, p], (up_dev, dn_dev)[way]).start()
+
+    def relay_when(where, q, way):
+        @pl.when(z == where)
+        def _():
+            relay(q, way)
 
     def pass_on(q, ways, p):
         if 0 in ways:
@@ -223,111 +206,163 @@
     for copy in right_loads:
         copy.start()
 
-    depth = X * rows
-    planewise = depth % PLANE_DEPTH == 0
     tile = min(ROW_TILE, block)
     tiles = block // tile
 
-    def multiply(q, stage):
-        plane = wbuf.at[q]
-
+    def multiply(j, xx, ps, stage, ks=tuple(range(K))):
         def one(i, carry):
-            k, at = i // tiles, pl.multiple_of(lax.rem(i, tiles) * tile, tile)
-            cols = pl.ds(pl.multiple_of(q * depth, depth), depth)
-            product = jnp.dot(
-                lbuf[k, pl.ds(at, tile), cols], plane[...].reshape(depth, block), preferred_element_type=F32
-            )
-            if stage == "only":
-                left[k, pl.ds(at, tile), :] = product.astype(BF16)
-            elif stage == "first":
-                acc[k, pl.ds(at, tile), :] = product
-            elif stage == "middle":
-                acc[k, pl.ds(at, tile), :] += product
-            else:
-                left[k, pl.ds(at, tile), :] = (acc[k, pl.ds(at, tile), :] + product).astype(BF16)
+            k, at = ks[0] + i // tiles, pl.multiple_of(lax.rem(i, tiles) * tile, tile)
+            sides = [
+                lbuf[k, pl.ds(at, tile), pl.ds(pl.multiple_of(((2 * j + n) * X + xx) * rows, rows), rows)]
+                for n in range(2)
+            ]
+            both = jnp.concatenate(sides, axis=1)
+            for p in ps:
+                product = jnp.dot(
+                    both, wbuf[xx, p, pl.ds(2 * j, 2)].reshape(2 * rows, width), preferred_element_type=F32
+                )
+                if stage == "first":
+                    acc[k, p, pl.ds(at, tile), :] = product
+                elif stage == "middle":
+                    acc[k, p, pl.ds(at, tile), :] += product
+                else:
+                    left[k, pl.ds(at, tile), pl.ds(p * width, width)] = (
+                        acc[k, p, pl.ds(at, tile), :] + product
+                    ).astype(BF16)
             return carry
 
-        lax.fori_loop(0, K * tiles, one, 0)
-
-    def take_plane(q, stage):
+        lax.fori_loop(0, len(ks) * tiles, one, 0)
+
+    def split_term(g, k, at, term):
+        psend[g, k, pl.ds(at, tile), :] = term[:, :LANES].astype(BF16)
+        own[g, k, pl.ds(at, tile), :] = term[:, LANES:]
+
+    def core_copy(g, k):
+        return remote(psend.at[g, k], precv.at[g, k], send_sem.at[1], recv_sem.at[1 + g], c_dev)
+
+    def first_second(h):
+        cols = pl.ds(h * block // 2, block // 2)
+
+        def one(i, carry):
+            at = pl.multiple_of(i * tile, tile)
+            for k in range(K):
+                term = lax.dot_general(
+                    left[k, pl.ds(at, tile), cols], rbuf[k, 0, :, :, cols].reshape(2 * LANES, block // 2),
+                    (((1,), (1,)), ((), ())), preferred_element_type=F32,
+                )
+                if h == 0:
+                    first_acc[k, pl.ds(at, tile), :] = term
+                else:
+                    split_term(0, k, at, first_acc[k, pl.ds(at, tile), :] + term)
+            return carry
+
+        lax.fori_loop(0, tiles, one, 0)
+        if h == 1:
+            for k in range(K):
+                core_copy(0, k).start()
+
+    def forward(d, p):
+        lo, hi = z - d, z + d
+
+        @pl.when(lo >= 0)
+        def _():
+            arrival(lo, x, p).wait_recv()
+            pass_on(lo, (0,), p)
+
+        @pl.when(hi < Z)
+        def _():
+            arrival(hi, x, p).wait_recv()
+            pass_on(hi, (1,), p)
+
+    def mirrored(q):
         for p in range(pieces):
             arrival(q, 1 - x, p).wait_recv()
-        if stage == "first":
-            relays_inward(lambda copy: copy.start())
-        if planewise:
-            multiply(q, stage)
 
     pltpu.make_async_copy(lbuf, lbuf, load_sem.at[0]).wait()
-
-    def forward(d, carry):
-        lo, hi = z - d, z + d
+    if nested:
+        near = z // 2
+        far = 1 - near
+        far_first = jnp.where(near == 0, 2, 1)
         for p in range(pieces):
-            @pl.when(lo >= 0)
-            def _():
-                arrival(lo, x, p).wait_recv()
-                pass_on(lo, (0,), p)
-
-            @pl.when(hi < Z)
-            def _():
-                arrival(hi, x, p).wait_recv()
-                pass_on(hi, (1,), p)
-
-        @pl.when(d == 1)
+            forward(1, p)
+        mirrored(z)
+        relay_when(0, 0, 0)
+        relay_when(3, 3, 1)
+        every = tuple(range(pieces))
+        halves = every[: pieces // 2], every[pieces // 2 :]
+        multiply(near, x, every, "first")
+        for p in every:
+            forward(2, p)
+        mirrored(4 * near + 1 - z)
+        for k in range(K):
+            multiply(near, 1 - x, every, "middle", (k,))
+            if k < 2:
+                for p in halves[0][k :: 2]:
+                    forward(3, p)
+        multiply(far, x, halves[0], "middle")
+        for p in halves[1]:
+            forward(3, p)
+        multiply(far, x, halves[1], "middle")
+        inner = (z == 1) | (z == 2)
+
+        @pl.when(inner)
         def _():
-            take_plane(z, "first")
-
-        return carry
-
-    if Z == 1:
-        take_plane(z, "only")
-    lax.fori_loop(1, Z, forward, 0)
-    relays_to_ends(lambda copy: copy.start())
-    near = jnp.minimum(z, Z - 1 - z)
-
-    def plane_by_distance(i):
-        d = (i + 1) // 2
-        both = jnp.where(lax.rem(i, 2) == 1, z - d, z + d)
-        return jnp.where(i <= 2 * near, both, jnp.where(z > near, z - (i - near), z + (i - near)))
-
-    def take_planes(i, carry):
-        take_plane(plane_by_distance(i), "middle")
-        return carry
-
-    lax.fori_loop(1, Z - 1, take_planes, 0)
-    if Z > 1:
-        take_plane(plane_by_distance(jnp.int32(Z - 1)), "last")
-
-    def whole_left(i, carry):
-        k, at = i // tiles, pl.multiple_of(lax.rem(i, tiles) * tile, tile)
-        value = jnp.dot(
-            lbuf[k, pl.ds(at, tile), :], wbuf[...].reshape(block, block), preferred_element_type=F32
-        )
-        left[k, pl.ds(at, tile), :] = value.astype(BF16)
-        return carry
-
-    if not planewise:
+            mirrored(far_first)
+
+        relay_when(1, 2, 1)
+        relay_when(2, 1, 0)
+        pltpu.make_async_copy(rbuf, rbuf, load_sem.at[1]).wait()
+        for h in range(2):
+            @pl.when(jnp.logical_not(inner))
+            def _(h=h):
+                for p in halves[h]:
+                    arrival(far_first, 1 - x, p).wait_recv()
+
+            for p in halves[h]:
+                arrival(4 * far + 1 - far_first, 1 - x, p).wait_recv()
+            multiply(far, 1 - x, halves[h], "last")
+            first_second(h)
+    else:
+        def forward_all(d, carry):
+            for p in range(pieces):
+                forward(d, p)
+            return carry
+
+        def mirrored_all(q, carry):
+            mirrored(q)
+            return carry
+
+        def whole_left(i, carry):
+            k, at = i // tiles, pl.multiple_of(lax.rem(i, tiles) * tile, tile)
+            for p in range(pieces):
+                value = jnp.dot(
+                    lbuf[k, pl.ds(at, tile), :], wbuf[p].reshape(block, width), preferred_element_type=F32
+                )
+                left[k, pl.ds(at, tile), pl.ds(p * width, width)] = value.astype(BF16)
+            return carry
+
+        lax.fori_loop(1, Z, forward_all, 0)
+        lax.fori_loop(0, Z, mirrored_all, 0)
         lax.fori_loop(0, K * tiles, whole_left, 0)
-    pltpu.make_async_copy(rbuf, rbuf, load_sem.at[1]).wait()
-
-    def core_copy(g, k):
-        return remote(psend.at[g, k], precv.at[g, k], send_sem.at[1], recv_sem.at[1 + g], c_dev)
+        pltpu.make_async_copy(rbuf, rbuf, load_sem.at[1]).wait()
 
     def core_arrival(g):
         return remote(psend.at[g], precv.at[g], send_sem.at[1], recv_sem.at[1 + g], c_dev)
 
-    def second(g, k):
+    def second(g):
         def one(i, carry):
             at = pl.multiple_of(i * tile, tile)
-            term = lax.dot_general(
-                left[k, pl.ds(at, tile), :], rbuf[k, g].reshape(2 * LANES, block),
-                (((1,), (1,)), ((), ())), preferred_element_type=F32,
-            )
-            psend[g, k, pl.ds(at, tile), :] = term[:, :LANES].astype(BF16)
-            own[g, k, pl.ds(at, tile), :] = term[:, LANES:]
+            for k in range(K):
+                term = lax.dot_general(
+                    left[k, pl.ds(at, tile), :], rbuf[k, g].reshape(2 * LANES, block),
+                    (((1,), (1,)), ((), ())), preferred_element_type=F32,
+                )
+                split_term(g, k, at, term)
             return carry
 
         lax.fori_loop(0, tiles, one, 0)
-        core_copy(g, k).start()
+        for k in range(K):
+            core_copy(g, k).start()
 
     def chip_sum(n, ty, zz, xx):
         unit = units[n]
@@ -511,15 +546,15 @@
             ready.add(g)
             core_arrival(g).wait_recv()
 
-    queue = [(g, k) for g in range(groups) for k in range(K)]
+    queue = list(range(1 if nested else 0, groups))
 
     def compute(count):
         for _ in range(min(count, len(queue))):
-            second(*queue.pop(0))
+            second(queue.pop(0))
 
     def start_pair(i):
         g = units[numbers[i][0]].group
-        while queue and queue[0][0] <= g:
+        while queue and queue[0] <= g:
             compute(1)
         receive(g)
         each(send, i)
@@ -528,24 +563,24 @@
     plain = [i for i in range(len(pairs)) if i != turned]
     steps = len(plain)
     done = set()
-    compute(K + 1)
+    compute(1 if nested else 2)
     weights_copy.wait_recv()
     start_pair(plain[0])
     start_pair(turned)
     start_pair(plain[1])
-    compute(K)
+    compute(1)
+    height = [units[numbers[i][0]].count for i in plain]
+    following = 2
     for j in range(steps):
         wait_pair(plain[j], 0)
         each(send_again, plain[j])
-        if j + 2 < steps:
-            start_pair(plain[j + 2])
+        while following < steps and following < j + 4:
+            start_pair(plain[following])
+            following += 1
             compute(1)
-        if j == max(0, steps - 3):
+        if j == steps - 1:
             wait_pair(turned, 0)
             each(send_again, turned)
-        if j == steps - 1:
-            wait_pair(turned, 1)
-            each(send_last, turned)
         if j >= 1:
             wait_pair(plain[j - 1], 1)
             each(send_last, plain[j - 1])
@@ -554,6 +589,8 @@
             done.add(1 + j - (steps - 2))
     wait_pair(plain[steps - 1], 1)
     each(send_last, plain[steps - 1])
+    wait_pair(turned, 1)
+    each(send_last, turned)
     for g in (*range(1, groups - 1), 0, groups - 1):
         if g not in done:
             done.add(g)
@@ -568,14 +605,15 @@
         def _(v=v):
             for way, count in ((0, v + 1 if v + 1 < Z else 0), (1, Z - v if v else 0)):
                 if count:
-                    span = wbuf.at[pl.ds(0, count), 0]
+                    span = left.at[0, pl.ds(0, count * rows)]
                     pltpu.make_async_copy(span, span, gat_s.at[way]).wait()
 
-    count = Z * rows - (piece if relayed else 0)
+    count = Z * rows - len(late) * rows // pieces
     flat = left.at[0, pl.ds(0, count)]
     pltpu.make_async_copy(flat, flat, gat_s.at[2]).wait()
-    relays_to_ends(lambda copy: copy.wait_send())
-    relays_inward(lambda copy: copy.wait_send())
+    if late:
+        flat = left.at[0, pl.ds(0, len(late) * rows // pieces)]
+        pltpu.make_async_copy(flat, flat, relay_s.at[0]).wait()
     weights_copy.wait_send()
     pltpu.make_async_copy(psend, psend, send_sem.at[1]).wait()
     pltpu.make_async_copy(xs, xs, send_sem.at[2]).wait()
@@ -598,7 +636,8 @@
         for unit in pair:
             heights = [height + size * unit.count for height, size in zip(heights, unit_sizes(unit, Z, X))]
     dma = pltpu.SemaphoreType.DMA
-    planewise = (X * rows) % PLANE_DEPTH == 0
+    nested = Z == 4 and rows % LANES == 0
+    width = block // PIECES
     hbm = pl.BlockSpec(memory_space=pltpu.HBM)
     operands = (
         wave[0], targets.reshape(-1), sector_sizes, pair_ids, pair_coefficients, left_ops[:, 0], right_ops[:, 0]
@@ -611,10 +650,11 @@
         scratch_shapes=[
             *(pltpu.SMEM(a.shape, a.dtype) for a in operands[1:5]),
             pltpu.VMEM((rows, block), BF16),
-            pltpu.VMEM((Z, X, rows, block), BF16),
+            pltpu.VMEM((X, PIECES, Z, rows, width) if nested else (PIECES, Z, X, rows, width), BF16),
             pltpu.VMEM((K, block, block), BF16),
             pltpu.VMEM((K, groups, 2, LANES, block), BF16),
-            pltpu.VMEM((K, block, block) if planewise else (8, LANES), F32),
+            pltpu.VMEM((K, PIECES, block, width) if nested else (8, LANES), F32),
+            pltpu.VMEM((K, block, 2 * LANES) if nested else (8, LANES), F32),
             pltpu.VMEM((K, block, block), BF16),
             pltpu.VMEM((groups, K, block, LANES), F32),
             pltpu.VMEM((groups, K, block, LANES), BF16),
@@ -625,7 +665,7 @@
             pltpu.VMEM((groups, rows, LANES), F32),
             *(pltpu.VMEM((height, LANES), BF16) for height in heights for _ in range(2)),
             dma((7,)), dma((6,)), dma((1 + 2 * groups,)), dma((len(pairs), 3)),
-            dma((3,)), dma((Z, X, PIECES)), dma((2,)),
+            dma((3,)), dma((Z, X, PIECES)), dma((1,)),
         ],
         compiler_params=pltpu.CompilerParams(
             collective_id=0, has_side_effects=True, vmem_limit_bytes=VMEM_LIMIT

time: 75.2 us -> 70.7 us (0.940)
  Pallas kernels: 74.3 us -> 69.8 us
    pallas_call x1, Pallas kernels: 74.3 us -> 69.8 us  [body(): pl.pallas_call(functools.partial(step_kernel, (Z, X, T, K, rows, block, g...]
where the time goes in v4:
time: 70.7 us; the launch traced here: 70.6 us
  Pallas kernels  69.8 us (99%)
  local copies, waits for them, and re-layouts  0.8 us (1%)
    pallas_call x1, Pallas kernels, body(): pl.pallas_call(functools.partial(step_kernel, (Z, X, T, K, rows, block, g...  69.8 us

profile of v4, /device:TPU:0, one launch (start us, length us, event | category | flops | bytes accessed | tf_op | source)
XLA Modules:
  0.0 70.6 jit_solution(4793469517945449437)
XLA Ops:
  0.0 69.8 %sigma_step.1 = f32[128,1024]{1,0:T(8,128)S(1)} custom-call(bf16[128,1024]{1,0:T(8,128)(2,1)} %bitcast.8, s32[2]{0:T(128)} %bitcast.9, s32[4]{0:T(128)} %sizes_hbm.1, s32[2]{0:T(128)} %ids_hbm.1, f32[16]{0:T(128)} %coefs_hbm.1, bf16[2,1024,1024]{2,1,0:T(8,128)(2,1)} %bitcast.6, bf16[2,1024,1024]{2,1,0:T(8,128)(2,1)} %bitcast.7), custom_call_target="tpu_custom_call" | custom-call | tf_op jit(solution)/shard_map/sigma_step/pallas_call | solution.py:645
  69.8 0.8 %copy.9 = f32[1,128,1024]{2,1,0:T(8,128)} copy(f32[1,128,1024]{2,1,0:T(8,128)S(1)} %bitcast.5) | data formatting | bytes 1048576

commit v5 on v4

--- a/solution.py
+++ b/solution.py
@@ -14,33 +14,41 @@
 ROW_TILE = 1024
 PIECES = 4
 VMEM_LIMIT = 48 * 1024 * 1024
+TURNED = (1, 3)
+MERGE_LAG = 3
 
 
 class Unit:
-    def __init__(self, group, core, start, count, order):
-        self.group, self.core, self.start, self.count, self.order = group, core, start, count, order
-
-
-def plan(groups, rows):
+    def __init__(self, group, core, start, count, order, merged):
+        self.group, self.core, self.start, self.count = group, core, start, count
+        self.order, self.merged = order, merged
+
+
+def plan(groups, rows, Z):
     pairs = []
     for g in range(groups):
-        parts = 1 if rows % 32 else 4 if g == groups - 1 and rows % 64 == 0 else 2
-        count = rows // parts
-        if parts == 1:
-            found = [[(g, tc, 0, rows) for tc in range(2)]]
-        else:
-            found = [
-                [(g, tc, (i + h) * count, count) for h in range(2)] for tc in range(2) for i in range(0, parts, 2)
-            ]
-        pairs += found
-    orders = [("zxy", "zyx") if n == 1 else ("xyz", "yxz") for n in range(len(pairs))]
-    return [[Unit(*part, order) for part, order in zip(pair, way)] for pair, way in zip(pairs, orders)]
+        if rows % 32:
+            pairs.append([(g, tc, 0, rows) for tc in range(2)])
+            continue
+        for tc in range(2):
+            small = rows % 64 == 0 and (g == groups - 1 or (g, tc) == (1, 1))
+            parts = 4 if small else 2
+            for i in range(0, parts, 2):
+                pairs.append([(g, tc, (i + h) * (rows // parts), rows // parts) for h in range(2)])
+    largest = max(pair[0][3] for pair in pairs)
+    found = []
+    for n, pair in enumerate(pairs):
+        turned = n in TURNED and len(pairs) > 2 * len(TURNED)
+        way = ("zxy", "zyx") if turned else ("xyz", "yxz")
+        merged = Z == 4 and not turned and pair[0][3] == largest
+        found.append([Unit(*part, order, merged) for part, order in zip(pair, way)])
+    return found
 
 
 def unit_sizes(unit, Z, X):
     return {
-        "xyz": (2 * Z, Z, Z),
-        "yxz": (Z, Z * X, Z),
+        "xyz": (2 * Z, Z, 6 if unit.merged else Z),
+        "yxz": (Z, Z * X, 6 if unit.merged else Z),
         "zxy": (2, 1, Z * 2 * X),
         "zyx": (1, X, Z * 2 * X),
     }[unit.order]
@@ -49,7 +57,7 @@
 def step_kernel(
     cfg, wave_hbm, targets_hbm, sizes_hbm, ids_hbm, coefs_hbm, left_hbm, right_hbm, out_ref,
     targets_ref, sizes_ref, ids_ref, coefs_ref,
-    wave_ref, wbuf, lbuf, rbuf, acc, first_acc, left, own, psend, precv, weight_ref, wother, fsend, frecv,
+    wave_ref, wbuf, lbuf, rbuf, acc, first_acc, left, own, psend, precv, weight_ref, wother, fsend, frecv, totals,
     xs, xr, ys, yr, zs, zr, load_sem, send_sem, recv_sem, pair_sem, gat_s, gat_r, relay_s,
 ):
     Z, X, T, K, rows, block, groups, pairs = cfg
@@ -58,6 +66,7 @@
     for unit in units:
         offsets.append(tuple(ends))
         ends = [end + size * unit.count for end, size in zip(ends, unit_sizes(unit, Z, X))]
+    grain = min(unit.count for unit in units)
     half = block // 2
     pair, sector = lax.axis_index("pair"), lax.axis_index("sector")
     z, x = pair // X, lax.rem(pair, X)
@@ -122,14 +131,17 @@
 
     def rows_of(n, axis, index):
         count = units[n].count
-        return pl.ds(pl.multiple_of(offsets[n][axis] + index * count, count), count)
+        return pl.ds(pl.multiple_of(offsets[n][axis] + index * count, grain), count)
 
     def z_index(n, zz, ty=0, xx=0):
         return zz if units[n].order[2] == "z" else (zz * 2 + ty) * X + xx
 
     for n, unit in enumerate(units):
+        if unit.merged:
+            zr[pl.ds(offsets[n][2] + 2 * unit.count, 2 * unit.count), :] = jnp.zeros((2 * unit.count, LANES), BF16)
+            continue
         size = unit_sizes(unit, Z, X)[2] // Z * unit.count
-        zr[pl.ds(pl.multiple_of(offsets[n][2] + z * size, unit.count), size), :] = jnp.zeros((size, LANES), BF16)
+        zr[pl.ds(pl.multiple_of(offsets[n][2] + z * size, grain), size), :] = jnp.zeros((size, LANES), BF16)
     for copy in left_loads:
         copy.start()
     for copy in small_loads:
@@ -401,15 +413,17 @@
         return remote(s.at[span], r.at[span], send_sem.at[2 + axis], pair_sem.at[pair_of[n], slot], device)
 
     def z_span(n, zz):
-        size = unit_sizes(units[n], Z, X)[2] // Z * units[n].count
-        return pl.ds(pl.multiple_of(offsets[n][2] + zz * size, units[n].count), size)
-
-    def line_slot(n):
-        return 2 if units[n].order[2] == "z" else 0
+        size = units[n].count * (1 if units[n].merged else unit_sizes(units[n], Z, X)[2] // Z)
+        return pl.ds(pl.multiple_of(offsets[n][2] + zz * size, grain), size)
 
     def line_copy(n, zz):
-        sem = pair_sem.at[pair_of[n], line_slot(n)]
+        sem = pair_sem.at[pair_of[n], 2 if units[n].order[2] == "z" else 0]
         return remote(zs.at[z_span(n, zz)], zr.at[z_span(n, z)], send_sem.at[4], sem, dev(zz=zz))
+
+    def merged_copy(n, mine, there, zz, slot):
+        return remote(
+            zs.at[z_span(n, mine)], zr.at[z_span(n, there)], send_sem.at[4], pair_sem.at[pair_of[n], slot], dev(zz=zz)
+        )
 
     def wait_rows(sem, count):
         if count:
@@ -419,9 +433,17 @@
         count = 0
         for n in numbers[i]:
             unit, sizes = units[n], unit_sizes(units[n], Z, X)
-            letter = unit.order[slot]
-            count += (sizes["xyz".index(letter)] // Z * (Z - 1) if letter == "z" else sizes["xyz".index(letter)]) * unit.count
+            if unit.merged and slot >= 2:
+                count += 2 * unit.count
+            elif unit.order[slot] == "z":
+                count += sizes[2] // Z * (Z - 1) * unit.count
+            else:
+                count += sizes["xy".index(unit.order[slot])] * unit.count
         wait_rows(pair_sem.at[i, slot], count)
+
+    at_end = (z == 0) | (z == Z - 1)
+    buddy = z + 1 - 2 * lax.rem(z, 2)
+    far_halves = ((2, 2 - z // 2), (3, 3 - 3 * (z // 2)))
 
     def others(f):
         loop(Z - 1, lambda j: f(lax.rem(z + 1 + j, Z)))
@@ -489,7 +511,18 @@
 
     def send_last(n):
         order = units[n].order
-        if order[2] == "z":
+        if units[n].merged:
+            put_z(n, 0, plane_sum(n, buddy))
+            for slot, zz in far_halves:
+                put_z(n, slot, plane_sum(n, zz))
+
+            @pl.when(at_end)
+            def _():
+                for slot, _ in far_halves:
+                    merged_copy(n, slot, slot, buddy, 3).start()
+
+            merged_copy(n, 0, 0, buddy, 2).start()
+        elif order[2] == "z":
             def one(zz):
                 put_z(n, zz, plane_sum(n, zz))
                 line_copy(n, zz).start()
@@ -502,8 +535,27 @@
             put_x(n, 0, summed(n, y, 1 - x) + from_y(n, 1 - x))
             step_copy(n, "x", 2).start()
 
+    def merge(i):
+        if not units[numbers[i][0]].merged:
+            return
+
+        @pl.when(jnp.logical_not(at_end))
+        def _():
+            wait_pair(i, 3)
+
+        for n in numbers[i]:
+            for slot, zz in far_halves:
+                put_z(n, slot + 2, plane_sum(n, zz) + from_z(n, slot))
+
+            @pl.when(jnp.logical_not(at_end))
+            def _(n=n):
+                for slot, zz in far_halves:
+                    merged_copy(n, slot + 2, 1, zz, 2).start()
+
     def total(n):
         order = units[n].order
+        if units[n].merged:
+            return plane_sum(n, z) + from_z(n, 0) + from_z(n, 1)
         if order[2] == "z":
             return line_sum(n, plane_sum(n, z))
         if order == "zxy":
@@ -524,15 +576,12 @@
         for i in range(len(pairs)):
             if units[numbers[i][0]].group == g:
                 wait_pair(i, 2)
-        here = [n for n in range(len(units)) if units[n].group == g]
-        for n in here:
-            if units[n].core == 0:
-                start, count = units[n].start, units[n].count
-                twin = [m for m in here if units[m].core == 1 and units[m].start == start]
-                one, two = total(n), total(twin[0])
-                span = pl.ds(start, count)
-                out_ref[span, pl.ds(at, LANES)] = jnp.where(c == 0, one, two) * used(at, start, count)
-                fsend[g, span, :] = jnp.where(c == 0, two, one)
+        for n, unit in enumerate(units):
+            if unit.group == g:
+                totals[unit.core, pl.ds(unit.start, unit.count), :] = total(n)
+        one, two = totals[0], totals[1]
+        out_ref[:, pl.ds(at, LANES)] = jnp.where(c == 0, one, two) * used(at)
+        fsend[g] = jnp.where(c == 0, two, one)
         final_copy(g).start()
 
     def each(f, i):
@@ -559,18 +608,16 @@
         receive(g)
         each(send, i)
 
-    turned = 1
-    plain = [i for i in range(len(pairs)) if i != turned]
+    turned = [i for i in range(len(pairs)) if units[numbers[i][0]].order[0] == "z"]
+    plain = [i for i in range(len(pairs)) if i not in turned]
     steps = len(plain)
     done = set()
     compute(1 if nested else 2)
     weights_copy.wait_recv()
-    start_pair(plain[0])
-    start_pair(turned)
-    start_pair(plain[1])
+    for i in range(min(len(pairs), 4)):
+        start_pair(i)
     compute(1)
-    height = [units[numbers[i][0]].count for i in plain]
-    following = 2
+    following = len([i for i in plain if i < 4])
     for j in range(steps):
         wait_pair(plain[j], 0)
         each(send_again, plain[j])
@@ -579,18 +626,21 @@
             following += 1
             compute(1)
         if j == steps - 1:
-            wait_pair(turned, 0)
-            each(send_again, turned)
+            for i in turned:
+                wait_pair(i, 0)
+                each(send_again, i)
         if j >= 1:
             wait_pair(plain[j - 1], 1)
             each(send_last, plain[j - 1])
-        if j >= steps - 2 and 1 + j - (steps - 2) < groups - 1:
-            finish(1 + j - (steps - 2))
-            done.add(1 + j - (steps - 2))
+        if j >= MERGE_LAG:
+            merge(plain[j - MERGE_LAG])
     wait_pair(plain[steps - 1], 1)
     each(send_last, plain[steps - 1])
-    wait_pair(turned, 1)
-    each(send_last, turned)
+    for j in range(max(0, steps - MERGE_LAG), steps):
+        merge(plain[j])
+    for i in turned:
+        wait_pair(i, 1)
+        each(send_last, i)
     for g in (*range(1, groups - 1), 0, groups - 1):
         if g not in done:
             done.add(g)
@@ -618,7 +668,10 @@
     pltpu.make_async_copy(psend, psend, send_sem.at[1]).wait()
     pltpu.make_async_copy(xs, xs, send_sem.at[2]).wait()
     pltpu.make_async_copy(ys, ys, send_sem.at[3]).wait()
-    wait_rows(send_sem.at[4], zs.shape[0] // Z * (Z - 1))
+    wait_rows(
+        send_sem.at[4],
+        sum(u.count * (3 if u.merged else unit_sizes(u, Z, X)[2] // Z * (Z - 1)) for u in units),
+    )
     pltpu.make_async_copy(fsend, fsend, send_sem.at[5]).wait()
 
 
@@ -630,7 +683,7 @@
     X = 2
     Z = lax.axis_size("pair") // X
     groups = block // 2 // LANES
-    pairs = plan(groups, rows)
+    pairs = plan(groups, rows, Z)
     heights = [0, 0, 0]
     for pair in pairs:
         for unit in pair:
@@ -663,8 +716,9 @@
             pltpu.VMEM((K * T, 8, LANES), F32),
             pltpu.VMEM((groups, rows, LANES), F32),
             pltpu.VMEM((groups, rows, LANES), F32),
+            pltpu.VMEM((2, rows, LANES), F32),
             *(pltpu.VMEM((height, LANES), BF16) for height in heights for _ in range(2)),
-            dma((7,)), dma((6,)), dma((1 + 2 * groups,)), dma((len(pairs), 3)),
+            dma((7,)), dma((6,)), dma((1 + 2 * groups,)), dma((len(pairs), 4)),
             dma((3,)), dma((Z, X, PIECES)), dma((1,)),
         ],
         compiler_params=pltpu.CompilerParams(

time: 70.7 us -> 69.3 us (0.980)
  Pallas kernels: 69.8 us -> 68.3 us
    pallas_call x1, Pallas kernels: 69.8 us -> 68.3 us  [body(): pl.pallas_call(functools.partial(step_kernel, (Z, X, T, K, rows, block, g...]
where the time goes in v5:
time: 69.3 us; the launch traced here: 69.1 us
  Pallas kernels  68.3 us (99%)
  local copies, waits for them, and re-layouts  0.8 us (1%)
    pallas_call x1, Pallas kernels, body(): pl.pallas_call(functools.partial(step_kernel, (Z, X, T, K, rows, block, g...  68.3 us

profile of v5, /device:TPU:0, one launch (start us, length us, event | category | flops | bytes accessed | tf_op | source)
XLA Modules:
  0.0 69.1 jit_solution(18342732712202768548)
XLA Ops:
  0.0 68.3 %sigma_step.1 = f32[128,1024]{1,0:T(8,128)S(1)} custom-call(bf16[128,1024]{1,0:T(8,128)(2,1)} %bitcast.8, s32[2]{0:T(128)} %bitcast.9, s32[4]{0:T(128)} %sizes_hbm.1, s32[2]{0:T(128)} %ids_hbm.1, f32[16]{0:T(128)} %coefs_hbm.1, bf16[2,1024,1024]{2,1,0:T(8,128)(2,1)} %bitcast.6, bf16[2,1024,1024]{2,1,0:T(8,128)(2,1)} %bitcast.7), custom_call_target="tpu_custom_call" | custom-call | tf_op jit(solution)/shard_map/sigma_step/pallas_call | solution.py:698
  68.3 0.8 %copy.9 = f32[1,128,1024]{2,1,0:T(8,128)} copy(f32[1,128,1024]{2,1,0:T(8,128)S(1)} %bitcast.5) | data formatting | bytes 1048576

commit v6 on v5

--- a/solution.py
+++ b/solution.py
@@ -14,7 +14,7 @@
 ROW_TILE = 1024
 PIECES = 4
 VMEM_LIMIT = 48 * 1024 * 1024
-TURNED = (1, 3)
+TURNED = (1, 3, 4)
 MERGE_LAG = 3
 
 
@@ -612,16 +612,16 @@
     plain = [i for i in range(len(pairs)) if i not in turned]
     steps = len(plain)
     done = set()
-    compute(1 if nested else 2)
+    compute(0 if nested else 2)
     weights_copy.wait_recv()
-    for i in range(min(len(pairs), 4)):
+    for i in range(min(len(pairs), 5)):
         start_pair(i)
     compute(1)
-    following = len([i for i in plain if i < 4])
+    following = len([i for i in plain if i < 5])
     for j in range(steps):
         wait_pair(plain[j], 0)
         each(send_again, plain[j])
-        while following < steps and following < j + 4:
+        while following < steps and following < j + 3:
             start_pair(plain[following])
             following += 1
             compute(1)

time: 69.3 us -> 67.5 us (0.974)
  Pallas kernels: 68.3 us -> 66.6 us
    pallas_call x1, Pallas kernels: 68.3 us -> 66.6 us  [body(): pl.pallas_call(functools.partial(step_kernel, (Z, X, T, K, rows, block, g...]
where the time goes in v6:
time: 67.5 us; the launch traced here: 67.4 us
  Pallas kernels  66.6 us (99%)
  local copies, waits for them, and re-layouts  0.8 us (1%)
    pallas_call x1, Pallas kernels, body(): pl.pallas_call(functools.partial(step_kernel, (Z, X, T, K, rows, block, g...  66.6 us

profile of v6, /device:TPU:0, one launch (start us, length us, event | category | flops | bytes accessed | tf_op | source)
XLA Modules:
  0.0 67.4 jit_solution(4276526225424330124)
XLA Ops:
  0.0 66.6 %sigma_step.1 = f32[128,1024]{1,0:T(8,128)S(1)} custom-call(bf16[128,1024]{1,0:T(8,128)(2,1)} %bitcast.8, s32[2]{0:T(128)} %bitcast.9, s32[4]{0:T(128)} %sizes_hbm.1, s32[2]{0:T(128)} %ids_hbm.1, f32[16]{0:T(128)} %coefs_hbm.1, bf16[2,1024,1024]{2,1,0:T(8,128)(2,1)} %bitcast.6, bf16[2,1024,1024]{2,1,0:T(8,128)(2,1)} %bitcast.7), custom_call_target="tpu_custom_call" | custom-call | tf_op jit(solution)/shard_map/sigma_step/pallas_call | solution.py:698
  66.6 0.8 %copy.9 = f32[1,128,1024]{2,1,0:T(8,128)} copy(f32[1,128,1024]{2,1,0:T(8,128)S(1)} %bitcast.5) | data formatting | bytes 1048576
